TPU v7x, 512 devices: a whole 4x4x16 slice. The times are simulated.
512 devices in a mesh: depth: 4 (over y_hi, core), blk: 128 (over z, x, y_lo).
Axes of the slice: x: 4, y: 4 (y_hi: 2, y_lo: 2; y = y_hi * 2 + y_lo), z: 16, core: 2. Of those that a mesh axis runs over, the one named last changes fastest.
Arguments:
- jacobian: bfloat16 [1536, 16384], P(('depth', 'blk')), may hold values from -6 to 6
- gain_inverse: bfloat16 [16384, 16384], P('depth', 'blk'), may hold values from -0.00024414062 to 0.00048828125, as said below
- variance: float32 [1536], P(('depth', 'blk')), may hold values from 2 to 12
Outputs:
- omega_diag: float32 [1536], P(('depth', 'blk'))
Inputs may be any that keep to these rules, and one draw needn't show every extreme that they name: gain_inverse is symmetric and positive definite.
All inputs are finite; a program needn't handle non-finite values.
Results may differ from a plain program's by a relative error of at most 0.0003.
Values may be sent and summed in bfloat16 or wider, within the bound.
No kernel may reach another device: no remote copies, remote signals or barrier semaphores. Data moves between devices by JAX's collectives and lax.ppermute only.
A program may use at most 128 MiB of HBM per device.

v0:
```python
import jax
import jax.numpy as jnp
from jax import lax
from jax.sharding import Mesh
from jax.sharding import PartitionSpec as P

BLK = ("blk_0", "blk_1", "blk_2")
DEPTH_BLK = ("depth", "blk_0", "blk_1", "blk_2")


def in_order(parts, dim):
    shape = list(parts.shape[1:])
    shape[dim] *= parts.shape[0]
    return jnp.moveaxis(parts, 0, dim).reshape(shape)


def copy_for_each(shard, axis):
    copies = jnp.broadcast_to(shard, (lax.axis_size(axis), *shard.shape))
    return lax.all_to_all(copies, axis, split_axis=0, concat_axis=0, tiled=True)


def collect(shard, axis, dim):
    return in_order(copy_for_each(shard, axis), dim)


def edges_of(length, count):
    unit = 8 if length >= 8 * count else 1
    return [length // unit * k // count * unit for k in range(1, count)]


def gather_in_order(shard, axes, turns):
    parts = shard[None]
    for k in turns:
        parts = lax.all_gather(parts, axes[k], axis=0, tiled=True)
    current = [lax.axis_size(axes[k]) for k in reversed(turns)]
    parts = parts.reshape(*current, *shard.shape)
    turned = sorted(range(len(turns)), key=lambda place: turns[len(turns) - 1 - place])
    return parts.transpose(*turned, *range(len(turns), parts.ndim)).reshape(-1, *shard.shape)


def gather_all_axes(shard, axes, dim):
    numbers = list(range(len(axes)))[::-1]
    cut = shard.shape.index(max(shard.shape[:-1] or shard.shape))
    edges = [0, *edges_of(shard.shape[cut], len(axes)), shard.shape[cut]]
    gathered = []
    for k, (start, end) in enumerate(zip(edges, edges[1:])):
        if end > start:
            slab = lax.slice_in_dim(shard, start, end, axis=cut)
            gathered.append(gather_in_order(slab, axes, numbers[k:] + numbers[:k]))
    return in_order(jnp.concatenate(gathered, axis=cut + 1), dim)


def shards(jacobian, gain_inverse, variance):
    rows_local = jacobian.shape[0]
    width = jacobian.shape[1]
    depth_count = lax.axis_size("depth")
    blk_count = lax.axis_size(BLK)
    panel_width = width // blk_count
    quarter_rows = lax.all_to_all(jacobian, "depth", split_axis=1, concat_axis=0, tiled=True)
    by_blk = lax.all_to_all(jacobian, BLK, split_axis=1, concat_axis=0, tiled=True)
    flat = by_blk.reshape(blk_count, rows_local * panel_width)
    joined = collect(flat, "depth", 1)
    panel = joined.reshape(blk_count * depth_count * rows_local, panel_width)
    gathered = gather_all_axes(quarter_rows, BLK, 0)
    projected = jnp.dot(gathered, gain_inverse, preferred_element_type=jnp.float32)
    partials = jnp.sum(projected * panel.astype(jnp.float32), axis=1)
    ordered = partials.reshape(blk_count, depth_count, rows_local).transpose(1, 0, 2).reshape(-1)
    quadratic = lax.psum_scatter(ordered, DEPTH_BLK, scatter_dimension=0, tiled=True)
    return variance - quadratic


def solution(mesh):
    split = Mesh(
        mesh.devices.reshape(mesh.shape["depth"], 16, 4, 2), ("depth", "blk_0", "blk_1", "blk_2")
    )
    return jax.shard_map(
        shards,
        mesh=split,
        in_specs=(P(DEPTH_BLK, None), P("depth", BLK), P(DEPTH_BLK)),
        out_specs=P(DEPTH_BLK),
        check_vma=False,
    )
```

profile of v0, /device:TPU:1, one launch (start us, length us, event | category | flops | bytes accessed | tf_op | source)
XLA Modules:
  0.0 513.9 jit_solution(17710025762078432333)
XLA Ops:
  6.5 0.0 copy-start
  6.5 0.0 all-gather.18.cloned.1.call-start
  6.5 15.3 %all_to_all.40 = bf16[3,4,4096]{2,0,1:T(4,128)(2,1)S(1)} all-to-all(bf16[3,4,4096]{2,0,1:T(4,128)(2,1)} %bitcast.30), channel_id=1, replica_groups=mesh['depth'=4,'blk_0'=16,'blk_1'=4,'blk_2'=2] {'depth'}, dimensions={1} | all-to-all | bytes 196608 | tf_op jit(solution)/shard_map/all_to_all | solution.py:59
  21.9 0.1 all_to_all.32
  22.0 29.5 %all-gather.5 = bf16[16,4,4096]{2,1,0:T(4,128)(2,1)} all-gather(bf16[1,4,4096]{2,1,0:T(4,128)(2,1)S(1)} %get-tuple-element.6), channel_id=4, replica_groups=mesh['depth'=4,'blk_0'=16,'blk_1'=4,'blk_2'=2] {'blk_0'}, dimensions={0}, use_global_device_ids=true | all-gather | bytes 557056 | tf_op jit(solution)/shard_map/all_gather | solution.py:34
  51.5 0.0 all-gather.18.cloned.1.call-update
  51.6 0.0 all-gather.14.cloned.1.call-start
  51.6 10.2 %all-gather.4 = bf16[4,4,4096]{2,1,0:T(4,128)(2,1)} all-gather(bf16[1,4,4096]{2,1,0:T(4,128)(2,1)S(1)} %get-tuple-element.7), channel_id=3, replica_groups=mesh['depth'=4,'blk_0'=16,'blk_1'=4,'blk_2'=2] {'blk_1'}, dimensions={0}, use_global_device_ids=true | all-gather | bytes 163840 | tf_op jit(solution)/shard_map/all_gather | solution.py:34
  61.8 0.0 all-gather.14.cloned.1.call-update
  61.8 0.0 all-gather.20.cloned.1.call-start
  61.9 21.9 %all-gather.18.cloned.1.call-done = bf16[32,4,4096]{2,1,0:T(4,128)(2,1)} async-done(((bf16[16,4,4096]{2,1,0:T(4,128)(2,1)}), bf16[32,4,4096]{2,1,0:T(4,128)(2,1)}) %all-gather.18.cloned.1.call-update) | async-done | bytes 1048592 | tf_op jit(solution)/shard_map/all_gather | solution.py:34
  83.7 0.0 all-gather.20.cloned.1.call-update
  83.8 0.0 all-gather.16.cloned.1.call-start
  83.8 66.7 %all-gather.14.cloned.1.call-done = bf16[64,4,4096]{2,1,0:T(4,128)(2,1)} async-done(((bf16[4,4,4096]{2,1,0:T(4,128)(2,1)}), bf16[64,4,4096]{2,1,0:T(4,128)(2,1)}) %all-gather.14.cloned.1.call-update) | async-done | bytes 2097168 | tf_op jit(solution)/shard_map/all_gather | solution.py:34
  150.5 0.0 all-gather.16.cloned.1.call-update
  150.5 0.0 all-gather.12.cloned.1.call-start
  150.6 3.7 all-gather.3
  154.2 10.6 %all_gather.28 = bf16[8,4,4096]{2,1,0:T(4,128)(2,1)} all-gather(bf16[2,4,4096]{2,1,0:T(4,128)(2,1)S(1)} %all-gather.3), channel_id=1, replica_groups=mesh['depth'=4,'blk_0'=16,'blk_1'=4,'blk_2'=2] {'blk_1'}, dimensions={0}, use_global_device_ids=true | all-gather | bytes 327680 | tf_op jit(solution)/shard_map/all_gather | solution.py:34
  164.8 0.0 all-gather.12.cloned.1.call-update
  164.8 26.2 %all_to_all.41 = bf16[3,128,128]{2,0,1:T(4,128)(2,1)S(1)} all-to-all(bf16[3,128,128]{2,0,1:T(4,128)(2,1)} %bitcast.31), channel_id=1, replica_groups=mesh['depth'=4,'blk_0'=16,'blk_1'=4,'blk_2'=2] {'blk_0','blk_1','blk_2'}, dimensions={1} | all-to-all | bytes 196608 | tf_op jit(solution)/shard_map/all_to_all | solution.py:60
  191.0 0.1 copy.23
  191.1 0.1 copy.24
  191.3 0.8 broadcast_in_dim.15
  192.1 19.0 %all-to-all-start.2 = ((bf16[4,128,384]{2,1,0:T(8,128)(2,1)}), bf16[4,128,384]{2,1,0:T(8,128)(2,1)S(1)}, u32[]{:S(2)}, u32[]{:S(2)}) async-start(bf16[4,128,384]{2,1,0:T(8,128)(2,1)} %broadcast_in_dim.15), calls=%async_computation.2 | async-start | bytes 786432 | tf_op jit(solution)/shard_map/all_to_all | solution.py:19
  211.0 7.9 %all-to-all-done.2 = bf16[4,128,384]{2,1,0:T(8,128)(2,1)S(1)} async-done(((bf16[4,128,384]{2,1,0:T(8,128)(2,1)}), bf16[4,128,384]{2,1,0:T(8,128)(2,1)S(1)}, u32[]{:S(2)}, u32[]{:S(2)}) %all-to-all-start.2) | async-done | bytes 393248 | tf_op jit(solution)/shard_map/all_to_all | solution.py:19
  219.0 0.1 convert_bitcast_fusion
  219.0 0.5 copy.25
  219.5 0.3 reshape.41
  219.9 0.3 copy.26
  220.1 0.0 all-gather.20.cloned.1.call-done
  220.2 7.9 %copy.21 = bf16[4,2,16,4,4096]{4,3,1,0,2:T(4,128)(2,1)} copy(bf16[4,2,16,4,4096]{4,3,2,1,0:T(4,128)(2,1)} %bitcast.27) | data formatting | bytes 8388608 | tf_op jit(solution)/shard_map/reshape | solution.py:36
  228.0 56.5 %all-gather.16.cloned.1.call-done = bf16[128,4,4096]{2,1,0:T(4,128)(2,1)} async-done(((bf16[64,4,4096]{2,1,0:T(4,128)(2,1)}), bf16[128,4,4096]{2,1,0:T(4,128)(2,1)}) %all-gather.16.cloned.1.call-update) | async-done | bytes 4194320 | tf_op jit(solution)/shard_map/all_gather | solution.py:34
  284.5 7.9 %copy.20 = bf16[2,16,4,4,4096]{4,3,0,2,1:T(4,128)(2,1)} copy(bf16[2,16,4,4,4096]{4,3,2,1,0:T(4,128)(2,1)} %bitcast.28) | data formatting | bytes 8388608 | tf_op jit(solution)/shard_map/reshape | solution.py:36
  292.4 64.5 %all-gather.12.cloned.1.call-done = bf16[128,4,4096]{2,1,0:T(4,128)(2,1)} async-done(((bf16[8,4,4096]{2,1,0:T(4,128)(2,1)}), bf16[128,4,4096]{2,1,0:T(4,128)(2,1)}) %all-gather.12.cloned.1.call-update) | async-done | bytes 4194320 | tf_op jit(solution)/shard_map/all_gather | solution.py:34
  356.9 12.1 %pad_maximum_fusion = bf16[128,12,4096]{2,1,0:T(8,128)(2,1)} fusion(bf16[128,4,4096]{2,1,0:T(4,128)(2,1)} %bitcast.25, bf16[128,4,4096]{2,1,0:T(4,128)(2,1)} %bitcast.26, bf16[128,4,4096]{2,1,0:T(4,128)(2,1)} %all-gather.12.cloned.1.call-done), kind=kLoop, calls=%fused_computation | loop fusion | flops 37748736 | bytes 25165824 | tf_op jit(solution)/shard_map/concatenate | solution.py:50
  369.0 18.1 %reshape.37 = bf16[1536,4096]{1,0:T(8,128)(2,1)} reshape(bf16[128,12,4096]{2,1,0:T(8,128)(2,1)} %pad_maximum_fusion) | data formatting | bytes 25165824 | tf_op jit(solution)/shard_map/reshape | solution.py:14
  387.1 0.0 copy-done
  387.1 0.0 copy-start.1
  387.1 8.9 %fusion = f32[1536]{0:T(1024)S(1)} fusion(f32[1536,128]{0,1:T(8,128)S(1)} %copy.26, bf16[1536,4096]{1,0:T(8,128)(2,1)} %reshape.37, bf16[4096,128]{1,0:T(8,128)(2,1)S(1)} %copy-done), kind=kOutput, calls=%fused_computation.2 | convolution fusion | flops 1611004416 | bytes 14424064 | tf_op jit(solution)/shard_map/dot_general | solution.py:65
  396.1 0.3 reshape.39
  396.4 0.2 reshape.40
  396.6 110.2 %all-reduce = f32[1536]{0:T(1024)S(1)} all-reduce(f32[1536]{0:T(1024)S(1)} %reshape.40), channel_id=5, replica_groups=mesh['depth'=4,'blk_0'=16,'blk_1'=4,'blk_2'=2] {'depth','blk_0','blk_1',..., use_global_device_ids=true, to_apply=%region_1.0.clone | all-reduce | flops 1536 | bytes 12288
  506.8 0.0 copy-done.1
  506.8 0.6 dynamic-slice_subtract_fusion
  (2 shorter events, 0.1 us)
Async XLA Ops:
  6.5 380.6 %copy-start = (bf16[4096,128]{1,0:T(8,128)(2,1)S(1)}, bf16[4096,128]{1,0:T(8,128)(2,1)}, u32[]{:S(2)}) copy-start(bf16[4096,128]{1,0:T(8,128)(2,1)} %param.4) | copy-start | bytes 3145732
  6.5 77.2 %all-gather.18.cloned.1.call-start = ((), (), s32[]{:S(2)}) async-start(), calls=%async_computation.6 | async-start | bytes 1572864 | tf_op jit(solution)/shard_map/all_gather | solution.py:34
  51.6 98.9 %all-gather.14.cloned.1.call-start = ((), (), s32[]{:S(2)}) async-start(), calls=%async_computation.4 | async-start | bytes 2228224 | tf_op jit(solution)/shard_map/all_gather | solution.py:34
  61.8 158.3 %all-gather.20.cloned.1.call-start = ((), (), s32[]{:S(2)}) async-start(), calls=%async_computation.7 | async-start | bytes 5242880 | tf_op jit(solution)/shard_map/all_gather | solution.py:34
  83.8 200.7 %all-gather.16.cloned.1.call-start = ((), (), s32[]{:S(2)}) async-start(), calls=%async_computation.5 | async-start | bytes 6291456 | tf_op jit(solution)/shard_map/all_gather | solution.py:34
  150.5 206.4 %all-gather.12.cloned.1.call-start = ((), (), s32[]{:S(2)}) async-start(), calls=%async_computation.3 | async-start | bytes 4456448 | tf_op jit(solution)/shard_map/all_gather | solution.py:34
  192.1 26.9 %all-to-all-start.2 = ((bf16[4,128,384]{2,1,0:T(8,128)(2,1)}), bf16[4,128,384]{2,1,0:T(8,128)(2,1)S(1)}, u32[]{:S(2)}, u32[]{:S(2)}) async-start(bf16[4,128,384]{2,1,0:T(8,128)(2,1)} %broadcast_in_dim.15), calls=%async_computation.2 | async-start | bytes 786432 | tf_op jit(solution)/shard_map/all_to_all | solution.py:19
  387.1 119.6 %copy-start.1 = (f32[3]{0:T(128)S(1)}, f32[3]{0:T(128)}, u32[]{:S(2)}) copy-start(f32[3]{0:T(128)} %param.5) | copy-start | bytes 40
Sparse Core Ops, SparseCore 0:
  51.7 32.0 all-gather.17
  85.8 64.6 all-gather.13
  152.6 63.1 all-gather.19
  217.7 66.7 all-gather.15
  286.4 70.4 all-gather.11
where the time goes:
time: 515 us; the launch traced here: 514 us
  waiting for transfers between devices  218 us (42%)
  blocking collectives  206 us (40%)
  local copies, waits for them, and re-layouts  36.6 us (7%)
  starting transfers between devices  19.1 us (4%)
  between operations  13.2 us (3%)
  other arithmetic  12.8 us (2%)
  matrix products  8.9 us (2%)
    all_gather x5, waiting for transfers between devices, gather_in_order(): parts = lax.all_gather(parts, axes[k], axis=0, tiled=True)  210 us
    unnamed x1, blocking collectives  110 us
    all_gather x4, blocking collectives, gather_in_order(): parts = lax.all_gather(parts, axes[k], axis=0, tiled=True)  54 us
    all_to_all x1, blocking collectives, shards(): lax.all_to_all(jacobian, BLK, split_axis=1, concat_axis=0, tiled=True)  26.2 us
    all_to_all x1, starting transfers between devices, copy_for_each(): return lax.all_to_all(copies, axis, split_axis=0, concat_axis=0, tiled=True)  19 us
    reshape x1, local copies, waits for them, and re-layouts, in_order(): return jnp.moveaxis(parts, 0, dim).reshape(shape)  18.1 us
    reshape x2, local copies, waits for them, and re-layouts, gather_in_order(): parts = parts.reshape(*current, *shard.shape)  15.7 us
    all_to_all x1, blocking collectives, shards(): lax.all_to_all(jacobian, 'depth', split_axis=1, concat_axis=0, tiled=True)  15.3 us
  transfers between devices with their start and end apart: 6, of which 5 were waited for; matrix products, arithmetic and copies ran while one was open for 3% of the time, Pallas kernels for 0%

commit v1 on v0

v1 whole, which is shorter than its diff:
```python
import functools

import jax
import jax.numpy as jnp
from jax import lax
from jax.experimental import pallas as pl
from jax.experimental.pallas import tpu as pltpu
from jax.sharding import Mesh
from jax.sharding import PartitionSpec as P

Z = "z"
PLANE = ("yh", "x", "yl")
ALL = ("yh", "core", "z", "x", "yl")
F32 = jnp.float32
BF16 = jnp.bfloat16
TILES = 16
LANES = 128
VMEM = pl.BlockSpec(memory_space=pltpu.VMEM)


def plane_index():
    return (lax.axis_index("yh") * lax.axis_size("x") + lax.axis_index("x")) * lax.axis_size(
        "yl"
    ) + lax.axis_index("yl")


def half_of(c, z):
    t = lax.rem(z - c + TILES, TILES)
    low = jnp.logical_or(t < TILES // 2, jnp.logical_and(t == TILES // 2, c < z))
    return jnp.where(low, 0, 1)


def exchange(parts, axis):
    return lax.all_to_all(parts, axis, split_axis=0, concat_axis=0, tiled=True)


def spread_kernel(rows, chunks, for_columns, in_ref, out_ref, wide):
    c = plane_index()
    z = lax.axis_index(Z)
    half = TILES // 2
    step = rows * chunks
    wide[...] = in_ref[...].astype(F32)
    mine = c if for_columns else z
    top = mine // half
    pieces = []
    for side in range(2):
        chunk_rows = []
        for q in range(chunks):
            base = side * half * step + q
            if for_columns:
                got = jnp.concatenate(
                    [
                        wide[pl.ds(base + r * chunks, half, stride=step), :]
                        for r in range(rows)
                    ],
                    axis=0,
                )
            else:
                got = wide[pl.ds(base, half * rows, stride=chunks), :]
            chunk_rows.append(got.astype(BF16))
        pieces.append(chunk_rows)
    for to in range(TILES):
        if for_columns:
            wanted = jnp.where(to == z, 1, half_of(to, z))
        else:
            wanted = half_of(c, to)
        first = (wanted + top) % 2 == 0

        @pl.when(first)
        def _():
            for q in range(chunks):
                out_ref[to, q] = pieces[0][q]

        @pl.when(jnp.logical_not(first))
        def _():
            for q in range(chunks):
                out_ref[to, q] = pieces[1][q]


def spread(parts, rows, chunks, for_columns):
    return pl.pallas_call(
        functools.partial(spread_kernel, rows, chunks, for_columns),
        out_shape=jax.ShapeDtypeStruct((TILES, chunks, TILES // 2 * rows, LANES), BF16),
        in_specs=[VMEM],
        out_specs=VMEM,
        scratch_shapes=[pltpu.VMEM((TILES * rows * chunks, LANES), F32)],
        cost_estimate=pl.CostEstimate(flops=2_000_000, bytes_accessed=900_000, transcendentals=0),
        name="spread_columns" if for_columns else "spread_rows",
    )(parts)


def tile_kernel(rows, chunks, x_ref, y_ref, own_ref, other_ref, out_ref, wide, left):
    c = plane_index()
    z = lax.axis_index(Z)
    core = lax.axis_index("core")
    half = TILES // 2
    group = half * rows
    total = TILES * group
    deep = chunks // 2 * LANES
    diagonal = c == z
    half_x = half_of(c, z)
    half_y = jnp.where(diagonal, 1, half_x)
    for j in range(chunks):
        for s in range(TILES):
            wide[j, s * group : (s + 1) * group, :] = y_ref[s, j].astype(F32)
    for q in range(chunks):
        side, lane = q // (chunks // 2), q % (chunks // 2) * LANES
        for s in range(TILES):
            left[side, s * group : (s + 1) * group, lane : lane + LANES] = x_ref[s, q]
            column_top = (half_y + s // half) % 2
            first = column_top * (half * group) + s % half
            got = wide[q, pl.ds(first, group, stride=half), :]
            left[side, total + s * group : total + (s + 1) * group, lane : lane + LANES] = got.astype(
                BF16
            )
    acc = jnp.zeros((2 * total, LANES), F32)
    for pair in range(chunks // 2):
        own = jnp.concatenate([own_ref[2 * pair], own_ref[2 * pair + 1]], axis=1)
        other = jnp.concatenate([other_ref[2 * pair], other_ref[2 * pair + 1]], axis=1)
        product = jnp.dot(left[core], own, preferred_element_type=F32)
        product += jnp.dot(left[1 - core], other, preferred_element_type=F32)
        side, lane = pair * 2 // (chunks // 2), pair * 2 % (chunks // 2) * LANES
        rows_x = left[side, :total, lane : lane + 2 * LANES].astype(F32)
        rows_y = left[side, total:, lane : lane + 2 * LANES].astype(F32)
        right = jnp.concatenate([jnp.where(diagonal, rows_x, rows_y), rows_y], axis=0)
        weighted = product * right
        acc += weighted[:, :LANES] + weighted[:, LANES:]
    ones = jnp.ones((8, LANES), F32)
    scale_x = jnp.where(diagonal, 1.0, 2.0)
    for s in range(TILES):
        sums = []
        for start in (s * group, total + s * group):
            sums.append(
                lax.dot_general(
                    ones,
                    acc[start : start + group],
                    (((1,), (1,)), ((), ())),
                    precision=lax.Precision.HIGHEST,
                    preferred_element_type=F32,
                )[:1]
            )
        from_x = sums[0] * scale_x
        from_y = jnp.where(diagonal, sums[1], 0.0)
        low = (half_x + s // half) % 2 == 0
        out_ref[s] = jnp.concatenate(
            [jnp.where(low, from_x, from_y), jnp.where(low, from_y, from_x)], axis=0
        )


def tile(x_rows, y_rows, own, other, rows, chunks):
    group = TILES // 2 * rows
    flops = 2 * 2 * TILES * group * (chunks * LANES) ** 2
    return pl.pallas_call(
        functools.partial(tile_kernel, rows, chunks),
        out_shape=jax.ShapeDtypeStruct((TILES, 2, group), F32),
        in_specs=[VMEM] * 4,
        out_specs=VMEM,
        scratch_shapes=[
            pltpu.VMEM((chunks, TILES * group, LANES), F32),
            pltpu.VMEM((2, 2 * TILES * group, chunks // 2 * LANES), BF16),
        ],
        cost_estimate=pl.CostEstimate(flops=flops, bytes_accessed=4_000_000, transcendentals=0),
        compiler_params=pltpu.CompilerParams(vmem_limit_bytes=48 * 1024 * 1024),
        name="tile",
    )(x_rows, y_rows, own, other)


def retile(gain):
    core = lax.axis_index("core")
    panel = gain.shape[1]
    halves = gain.reshape(TILES // 4, 2, -1, panel)
    kept = lax.dynamic_index_in_dim(halves, core, 1, keepdims=False)
    given = lax.dynamic_index_in_dim(halves, 1 - core, 1, keepdims=False)
    swap = [(0, 1), (1, 0)]
    taken = lax.ppermute(given, "core", swap)
    first = jnp.where(core == 0, kept, taken)
    second = jnp.where(core == 0, taken, kept)
    own = exchange(jnp.concatenate([first, second], axis=0), ("x", "yl"))
    return own, lax.ppermute(own, "core", swap)


def shards(jacobian, gain, variance):
    rows, width = jacobian.shape
    chunks = width // TILES // LANES
    parts = jacobian.reshape(rows, TILES, chunks, LANES).transpose(1, 0, 2, 3)
    parts = parts.reshape(TILES * rows * chunks, LANES)
    by_rows = exchange(parts, PLANE)
    by_columns = exchange(parts, Z)
    x_rows = exchange(spread(by_rows, rows, chunks, False), Z)
    y_rows = exchange(spread(by_columns, rows, chunks, True), PLANE)
    own, other = retile(gain)
    partial = tile(x_rows, y_rows, own, other, rows, chunks)
    along_z = exchange(partial, Z).sum(axis=0)
    in_plane = exchange(along_z.reshape(TILES, rows), PLANE).sum(axis=0)
    return variance - in_plane


def solution(mesh):
    devices = mesh.devices.reshape(2, 2, TILES, 4, 2)
    return jax.shard_map(
        shards,
        mesh=Mesh(devices, ALL),
        in_specs=(P(ALL, None), P(("yh", "core"), ("z", "x", "yl")), P(ALL)),
        out_specs=P(ALL),
        check_vma=False,
    )
```

time: 515 us -> 157 us (0.30)
  blocking collectives: 206 us -> 38.1 us
  waiting for transfers between devices: 218 us -> 54.9 us
  local copies, waits for them, and re-layouts: 36.6 us -> 6.17 us
  starting transfers between devices: 19.1 us -> 46.5 us
  between operations: 13.2 us -> 0.13 us
  other arithmetic: 12.8 us -> 1.71 us
  matrix products: 8.9 us -> 0 us
  Pallas kernels: 0 us -> 7.39 us
    all_gather x5 -> x0, waiting for transfers between devices: 210 us -> none  [gather_in_order(): parts = lax.all_gather(parts, axes[k], axis=0, tiled=True)]
    unnamed x1 -> x0, blocking collectives: 110 us -> none
    all_gather x4 -> x0, blocking collectives: 54 us -> none  [gather_in_order(): parts = lax.all_gather(parts, axes[k], axis=0, tiled=True)]
    all_to_all x1 -> x5, waiting for transfers between devices: 7.95 us -> 52.6 us  [exchange(): return lax.all_to_all(parts, axis, split_axis=0, concat_axis=0, tiled=True)]
    reshape x6 -> x0, local copies, waits for them, and re-layouts: 34.5 us -> none  [the longest x1 18.1 us: in_order(): return jnp.moveaxis(parts, 0, dim).reshape(shape)]
    all_to_all x1 -> x5, starting transfers between devices: 19 us -> 37.6 us  [exchange(): return lax.all_to_all(parts, axis, split_axis=0, concat_axis=0, tiled=True)]
    concatenate x1, other arithmetic: 12.1 us -> 1.06 us  [retile(): own = exchange(jnp.concatenate([first, second], axis=0), ('x', 'yl'))]
    ppermute x0 -> x2, starting transfers between devices: none -> 8.96 us  [the longest x1 6.1 us: retile(): return (own, lax.ppermute(own, 'core', swap))]
  transfers between devices with their start and end apart: 6 -> 7, of which waited for: 5 -> 6; matrix products, arithmetic and copies ran while one was open for 3% -> 1% of each run, Pallas kernels for 0% -> 3%
where the time goes in v1:
time: 157 us; the launch traced here: 155 us
  waiting for transfers between devices  54.9 us (35%)
  starting transfers between devices  46.5 us (30%)
  blocking collectives  38.1 us (24%)
  Pallas kernels  7.39 us (5%)
  local copies, waits for them, and re-layouts  6.17 us (4%)
  other arithmetic  1.71 us (1%)
    all_to_all x5, waiting for transfers between devices, exchange(): return lax.all_to_all(parts, axis, split_axis=0, concat_axis=0, tiled=True)  52.6 us
    all_to_all x2, blocking collectives, exchange(): return lax.all_to_all(parts, axis, split_axis=0, concat_axis=0, tiled=True)  38.1 us
    all_to_all x5, starting transfers between devices, exchange(): return lax.all_to_all(parts, axis, split_axis=0, concat_axis=0, tiled=True)  37.6 us
    ppermute x1, starting transfers between devices, retile(): return (own, lax.ppermute(own, 'core', swap))  6.1 us
    pallas_call x2, Pallas kernels, spread(): pl.pallas_call(functools.partial(spread_kernel, rows, chunks, for_columns...  4.48 us
    unnamed x12, local copies, waits for them, and re-layouts  3.46 us
  transfers between devices with their start and end apart: 7, of which 6 were waited for; matrix products, arithmetic and copies ran while one was open for 1% of the time, Pallas kernels for 3%

profile of v1, /device:TPU:1, one launch (start us, length us, event | category | flops | bytes accessed | tf_op | source)
XLA Modules:
  0.0 155.0 jit_solution(6869850003485870382)
XLA Ops:
  0.0 1.5 copy_bitcast_fusion
  1.5 15.7 %all-to-all-start.2 = ((bf16[16,24,128]{2,1,0:T(8,128)(2,1)}), bf16[16,24,128]{2,1,0:T(8,128)(2,1)S(1)}, u32[]{:S(2)}, u32[]{:S(2)}) async-start(bf16[16,24,128]{2,1,0:T(8,128)(2,1)} %copy_bitcast_fusion), calls=%async_computation.2 | async-start | bytes 196608 | tf_op jit(solution)/shard_map/all_to_all | solution.py:34
  17.3 1.1 dynamic-slice_bitcast_fusion
  18.4 2.9 %collective-permute-start = (bf16[4,512,128]{2,1,0:T(8,128)(2,1)S(1)}, bf16[4,512,128]{2,1,0:T(8,128)(2,1)S(1)}, u32[]{:S(2)}, u32[]{:S(2)}) collective-permute-start(bf16[4,512,128]{2,1,0:T(8,128)(2,1)S(1)} %dynamic-slice_bitcast_fusion), channel_id=1, source_target_pairs={{0,128},{128,0},{1,129},{129,1},{2,130},{130,2},{3,131},{131,3},{4... | collective-permute-start | bytes 1572872 | tf_op jit(solution)/shard_map/ppermute | solution.py:175
  21.3 7.9 %all-to-all-done.2 = bf16[16,24,128]{2,1,0:T(8,128)(2,1)S(1)} async-done(((bf16[16,24,128]{2,1,0:T(8,128)(2,1)}), bf16[16,24,128]{2,1,0:T(8,128)(2,1)S(1)}, u32[]{:S(2)}, u32[]{:S(2)}) %all-to-all-start.2) | async-done | bytes 98336 | tf_op jit(solution)/shard_map/all_to_all | solution.py:34
  29.1 0.0 copy-start.4
  29.1 6.8 %all-to-all-start = ((bf16[16,24,128]{2,1,0:T(8,128)(2,1)}), bf16[16,24,128]{2,1,0:T(8,128)(2,1)S(1)}, u32[]{:S(2)}, u32[]{:S(2)}) async-start(bf16[16,24,128]{2,1,0:T(8,128)(2,1)} %copy_bitcast_fusion), calls=%async_computation | async-start | bytes 196608 | tf_op jit(solution)/shard_map/all_to_all | solution.py:34
  35.9 0.0 copy-done.4
  35.9 0.0 copy-start.2
  35.9 2.3 %spread_columns.1 = bf16[16,8,24,128]{3,2,1,0:T(8,128)(2,1)} custom-call(bf16[384,128]{1,0:T(8,128)(2,1)} %bitcast.26), custom_call_target="tpu_custom_call" | custom-call | flops 2000000 | bytes 900000 | tf_op jit(solution)/shard_map/spread_columns/pallas_call | solution.py:81
  38.2 4.2 %all-to-all-done = bf16[16,24,128]{2,1,0:T(8,128)(2,1)S(1)} async-done(((bf16[16,24,128]{2,1,0:T(8,128)(2,1)}), bf16[16,24,128]{2,1,0:T(8,128)(2,1)S(1)}, u32[]{:S(2)}, u32[]{:S(2)}) %all-to-all-start) | async-done | bytes 98336 | tf_op jit(solution)/shard_map/all_to_all | solution.py:34
  42.4 0.0 copy-start.3
  42.4 0.6 copy-done.3
  43.1 3.6 %all-to-all-start.3 = ((bf16[16,8,24,128]{3,2,1,0:T(8,128)(2,1)}), bf16[16,8,24,128]{3,2,1,0:T(8,128)(2,1)S(1)}, u32[]{:S(2)}, u32[]{:S(2)}) async-start(bf16[16,8,24,128]{3,2,1,0:T(8,128)(2,1)} %spread_columns.1), calls=%async_computation.3 | async-start | bytes 1572864 | tf_op jit(solution)/shard_map/all_to_all | solution.py:34
  46.7 0.0 collective-permute-done
  46.7 0.0 copy-done.2
  46.7 0.1 bitcast_select_fusion.1
  46.8 1.1 pad_maximum_fusion
  47.9 9.5 %all-to-all-done.3.y_ref = bf16[16,8,24,128]{3,2,1,0:T(8,128)(2,1)S(1)} async-done(((bf16[16,8,24,128]{3,2,1,0:T(8,128)(2,1)}), bf16[16,8,24,128]{3,2,1,0:T(8,128)(2,1)S(1)}, u32[]{:S(2)}, u32[]{:S(2)}) %all-to-all-start.3) | async-done | bytes 786464 | tf_op jit(solution)/shard_map/all_to_all | solution.py:34
  57.4 3.6 %all-to-all-start.4 = ((bf16[8,512,128]{2,1,0:T(8,128)(2,1)}), bf16[8,512,128]{2,1,0:T(8,128)(2,1)S(1)}, u32[]{:S(2)}, u32[]{:S(2)}) async-start(bf16[8,512,128]{2,1,0:T(8,128)(2,1)} %pad_maximum_fusion), calls=%async_computation.4 | async-start | bytes 2097152 | tf_op jit(solution)/shard_map/all_to_all | solution.py:34
  61.0 2.2 %spread_rows.1 = bf16[16,8,24,128]{3,2,1,0:T(8,128)(2,1)} custom-call(bf16[384,128]{1,0:T(8,128)(2,1)} %bitcast.25), custom_call_target="tpu_custom_call" | custom-call | flops 2000000 | bytes 900000 | tf_op jit(solution)/shard_map/spread_rows/pallas_call | solution.py:81
  63.2 8.9 %all-to-all-done.4.own_ref = bf16[8,512,128]{2,1,0:T(8,128)(2,1)S(1)} async-done(((bf16[8,512,128]{2,1,0:T(8,128)(2,1)}), bf16[8,512,128]{2,1,0:T(8,128)(2,1)S(1)}, u32[]{:S(2)}, u32[]{:S(2)}) %all-to-all-start.4) | async-done | bytes 1048608 | tf_op jit(solution)/shard_map/all_to_all | solution.py:34
  72.1 7.9 %all-to-all-start.1 = ((bf16[16,8,24,128]{3,2,1,0:T(8,128)(2,1)}), bf16[16,8,24,128]{3,2,1,0:T(8,128)(2,1)S(1)}, u32[]{:S(2)}, u32[]{:S(2)}) async-start(bf16[16,8,24,128]{3,2,1,0:T(8,128)(2,1)} %spread_rows.1), calls=%async_computation.1 | async-start | bytes 1572864 | tf_op jit(solution)/shard_map/all_to_all | solution.py:34
  80.0 6.1 %collective-permute-start.1 = (bf16[8,512,128]{2,1,0:T(8,128)(2,1)S(1)}, bf16[8,512,128]{2,1,0:T(8,128)(2,1)S(1)}, u32[]{:S(2)}, u32[]{:S(2)}) collective-permute-start(bf16[8,512,128]{2,1,0:T(8,128)(2,1)S(1)} %all-to-all-done.4.own_ref), channel_id=1, source_target_pairs={{0,128},{128,0},{1,129},{129,1},{2,130},{130,2},{3,131},{131,3},{4... | collective-permute-start | bytes 3145736 | tf_op jit(solution)/shard_map/ppermute | solution.py:179
  86.1 2.3 %collective-permute-done.1.other_ref = bf16[8,512,128]{2,1,0:T(8,128)(2,1)S(1)} collective-permute-done((bf16[8,512,128]{2,1,0:T(8,128)(2,1)S(1)}, bf16[8,512,128]{2,1,0:T(8,128)(2,1)S(1)}, u32[]{:S(2)}, u32[]{:S(2)}) %collective-permute-start.1) | collective-permute-done | bytes 1048608 | tf_op jit(solution)/shard_map/ppermute | solution.py:179
  88.4 0.0 copy-start
  88.4 1.0 copy-done
  89.3 22.1 %all-to-all-done.1.x_ref = bf16[16,8,24,128]{3,2,1,0:T(8,128)(2,1)S(1)} async-done(((bf16[16,8,24,128]{3,2,1,0:T(8,128)(2,1)}), bf16[16,8,24,128]{3,2,1,0:T(8,128)(2,1)S(1)}, u32[]{:S(2)}, u32[]{:S(2)}) %all-to-all-start.1) | async-done | bytes 786464 | tf_op jit(solution)/shard_map/all_to_all | solution.py:34
  111.4 0.0 copy-start.1
  111.4 1.2 copy-done.1
  112.6 2.9 %tile.1 = f32[16,2,24]{2,1,0:T(2,128)S(1)} custom-call(bf16[16,8,24,128]{3,2,1,0:T(8,128)(2,1)S(1)} %all-to-all-done.1.x_ref, bf16[16,8,24,128]{3,2,1,0:T(8,128)(2,1)S(1)} %all-to-all-done.3.y_ref, bf16[8,512,128]{2,1,0:T(8,128)(2,1)S(1)} %all-to-all-done.4.own_ref, bf16[8,512,128]{2,1,0:T(8,128)(2,1)S(1)} %copy-done.1), custom_call_target="tpu_custom_call" | custom-call | flops 1610612736 | bytes 4000000 | tf_op jit(solution)/shard_map/tile/pallas_call | solution.py:153
  115.5 26.0 %all_to_all.48 = f32[16,2,24]{2,1,0:T(2,128)S(1)} all-to-all(f32[16,2,24]{2,1,0:T(2,128)S(1)} %tile.1), channel_id=1, replica_groups=mesh['yh'=2,'core'=2,'z'=16,'x'=4,'yl'=2] {'z'}, dimensions={0} | all-to-all | bytes 6144 | tf_op jit(solution)/shard_map/all_to_all | solution.py:34
  141.6 0.1 all_to_all.39
  141.6 12.1 %all_to_all.49 = f32[16,1,3]{2,1,0:T(1,128)S(1)} all-to-all(f32[16,1,3]{2,1,0:T(1,128)S(1)} %bitcast.28), channel_id=1, replica_groups=mesh['yh'=2,'core'=2,'z'=16,'x'=4,'yl'=2] {'yh','x','yl'}, dimensions={0} | all-to-all | bytes 384 | tf_op jit(solution)/shard_map/all_to_all | solution.py:34
  153.8 0.0 copy-start.5
  153.8 0.6 copy-done.5
  154.4 0.5 sub.7
  (2 shorter events, 0.1 us)
Async XLA Ops:
  1.5 27.6 %all-to-all-start.2 = ((bf16[16,24,128]{2,1,0:T(8,128)(2,1)}), bf16[16,24,128]{2,1,0:T(8,128)(2,1)S(1)}, u32[]{:S(2)}, u32[]{:S(2)}) async-start(bf16[16,24,128]{2,1,0:T(8,128)(2,1)} %copy_bitcast_fusion), calls=%async_computation.2 | async-start | bytes 196608 | tf_op jit(solution)/shard_map/all_to_all | solution.py:34
  18.4 28.3 %collective-permute-start = (bf16[4,512,128]{2,1,0:T(8,128)(2,1)S(1)}, bf16[4,512,128]{2,1,0:T(8,128)(2,1)S(1)}, u32[]{:S(2)}, u32[]{:S(2)}) collective-permute-start(bf16[4,512,128]{2,1,0:T(8,128)(2,1)S(1)} %dynamic-slice_bitcast_fusion), channel_id=1, source_target_pairs={{0,128},{128,0},{1,129},{129,1},{2,130},{130,2},{3,131},{131,3},{4... | collective-permute-start | bytes 1572872 | tf_op jit(solution)/shard_map/ppermute | solution.py:175
  29.1 6.8 %copy-start.4 = (bf16[16,24,128]{2,1,0:T(8,128)(2,1)}, bf16[16,24,128]{2,1,0:T(8,128)(2,1)S(1)}, u32[]{:S(2)}) copy-start(bf16[16,24,128]{2,1,0:T(8,128)(2,1)S(1)} %all-to-all-done.2) | copy-start | bytes 294916
  29.1 13.3 %all-to-all-start = ((bf16[16,24,128]{2,1,0:T(8,128)(2,1)}), bf16[16,24,128]{2,1,0:T(8,128)(2,1)S(1)}, u32[]{:S(2)}, u32[]{:S(2)}) async-start(bf16[16,24,128]{2,1,0:T(8,128)(2,1)} %copy_bitcast_fusion), calls=%async_computation | async-start | bytes 196608 | tf_op jit(solution)/shard_map/all_to_all | solution.py:34
  35.9 10.8 %copy-start.2 = (bf16[4096,128]{1,0:T(8,128)(2,1)S(1)}, bf16[4096,128]{1,0:T(8,128)(2,1)}, u32[]{:S(2)}) copy-start(bf16[4096,128]{1,0:T(8,128)(2,1)} %param.4) | copy-start | bytes 3145732
  42.4 0.6 copy-start.3
  43.1 14.3 %all-to-all-start.3 = ((bf16[16,8,24,128]{3,2,1,0:T(8,128)(2,1)}), bf16[16,8,24,128]{3,2,1,0:T(8,128)(2,1)S(1)}, u32[]{:S(2)}, u32[]{:S(2)}) async-start(bf16[16,8,24,128]{3,2,1,0:T(8,128)(2,1)} %spread_columns.1), calls=%async_computation.3 | async-start | bytes 1572864 | tf_op jit(solution)/shard_map/all_to_all | solution.py:34
  57.4 14.7 %all-to-all-start.4 = ((bf16[8,512,128]{2,1,0:T(8,128)(2,1)}), bf16[8,512,128]{2,1,0:T(8,128)(2,1)S(1)}, u32[]{:S(2)}, u32[]{:S(2)}) async-start(bf16[8,512,128]{2,1,0:T(8,128)(2,1)} %pad_maximum_fusion), calls=%async_computation.4 | async-start | bytes 2097152 | tf_op jit(solution)/shard_map/all_to_all | solution.py:34
  72.1 39.3 %all-to-all-start.1 = ((bf16[16,8,24,128]{3,2,1,0:T(8,128)(2,1)}), bf16[16,8,24,128]{3,2,1,0:T(8,128)(2,1)S(1)}, u32[]{:S(2)}, u32[]{:S(2)}) async-start(bf16[16,8,24,128]{3,2,1,0:T(8,128)(2,1)} %spread_rows.1), calls=%async_computation.1 | async-start | bytes 1572864 | tf_op jit(solution)/shard_map/all_to_all | solution.py:34
  80.0 8.4 %collective-permute-start.1 = (bf16[8,512,128]{2,1,0:T(8,128)(2,1)S(1)}, bf16[8,512,128]{2,1,0:T(8,128)(2,1)S(1)}, u32[]{:S(2)}, u32[]{:S(2)}) collective-permute-start(bf16[8,512,128]{2,1,0:T(8,128)(2,1)S(1)} %all-to-all-done.4.own_ref), channel_id=1, source_target_pairs={{0,128},{128,0},{1,129},{129,1},{2,130},{130,2},{3,131},{131,3},{4... | collective-permute-start | bytes 3145736 | tf_op jit(solution)/shard_map/ppermute | solution.py:179
  88.4 1.0 copy-start
  111.4 1.2 copy-start.1
  153.8 0.7 copy-start.5

commit v2 on v0

v2 whole, which is shorter than its diff:
```python
import functools

import jax
import jax.numpy as jnp
from jax import lax
from jax.experimental import pallas as pl
from jax.experimental.pallas import tpu as pltpu
from jax.sharding import Mesh
from jax.sharding import PartitionSpec as P

PLANE = ("yh", "x", "yl")
ALL = ("yh", "core", "z", "x", "yl")
F32 = jnp.float32
BF16 = jnp.bfloat16
TILES = 16
HALF = TILES // 2
LANES = 128
VMEM = pl.BlockSpec(memory_space=pltpu.VMEM)


def plane_index():
    return (lax.axis_index("yh") * 4 + lax.axis_index("x")) * 2 + lax.axis_index("yl")


def half_of(c, z):
    t = lax.rem(z - c + TILES, TILES)
    high = jnp.where(z >= HALF, 1, 0)
    return jnp.where(t == 0, high, jnp.where(t == HALF, 1 - high, jnp.where(t < HALF, 0, 1)))


def slot_of(c, z):
    t = lax.rem(z - c + TILES, TILES)
    high = jnp.where(z >= HALF, 1, 0)
    slot = jnp.where(half_of(c, z) == 0, t - high, TILES - t - (1 - high))
    return jnp.where(t == 0, HALF, slot)


def exchange(parts, axis):
    return lax.all_to_all(parts, axis, split_axis=0, concat_axis=0, tiled=True)


def pick_kernel(in_ref, out_ref):
    half = lax.rem(lax.axis_index("yh") + lax.axis_index("z") // HALF, 2)
    for z in range(TILES):
        high = 1 if z >= HALF else 0
        for slot in range(HALF):
            first = (z - slot - high) % TILES
            second = (z + slot + 1 - high) % TILES
            out_ref[z, slot] = in_ref[jnp.where(half == 0, first, second)]
        out_ref[z, HALF] = in_ref[z]


def pick(parts):
    return pl.pallas_call(
        pick_kernel,
        out_shape=jax.ShapeDtypeStruct((TILES, HALF + 1, *parts.shape[1:]), BF16),
        in_specs=[VMEM],
        out_specs=VMEM,
        cost_estimate=pl.CostEstimate(flops=1_000_000, bytes_accessed=900_000, transcendentals=0),
        compiler_params=pltpu.CompilerParams(vmem_limit_bytes=4 * 1024 * 1024),
        name="pick",
    )(parts)


def spread_kernel(rows, chunks, in_ref, out_ref, wide):
    z = lax.axis_index("z")
    top = lax.axis_index("yh")
    block = rows * chunks
    step = (HALF + 1) * block
    for s in range(TILES):
        wide[s * step : (s + 1) * step, :] = in_ref[s].astype(F32)

    @pl.loop(0, TILES)
    def _(to):
        half_x = half_of(to, z)
        half_y = jnp.where(to == z, 1 - half_x, half_x)
        base_x = lax.rem(half_x + top, 2) * (HALF * step) + slot_of(to, z) * block
        base_y = lax.rem(half_y + top, 2) * (HALF * step) + HALF * block
        for side, base in ((0, base_x), (1, base_y)):
            for q in range(chunks):
                got = [
                    wide[pl.ds(base + r * chunks + q, HALF, stride=step), :] for r in range(rows)
                ]
                out_ref[to, side * chunks + q] = jnp.concatenate(got, axis=0).astype(BF16)


def spread(parts, rows, chunks):
    return pl.pallas_call(
        functools.partial(spread_kernel, rows, chunks),
        out_shape=jax.ShapeDtypeStruct((TILES, 2 * chunks, HALF * rows, LANES), BF16),
        in_specs=[VMEM],
        out_specs=VMEM,
        scratch_shapes=[pltpu.VMEM((TILES * parts.shape[1], LANES), F32)],
        cost_estimate=pl.CostEstimate(flops=4_000_000, bytes_accessed=2_500_000, transcendentals=0),
        compiler_params=pltpu.CompilerParams(vmem_limit_bytes=8 * 1024 * 1024),
        name="spread",
    )(parts)


def tile_kernel(rows, chunks, xy_ref, own_ref, other_ref, out_ref, narrow, left):
    z = lax.axis_index("z")
    x = lax.axis_index("x")
    yl = lax.axis_index("yl")
    core = lax.axis_index("core")
    c = plane_index()
    group = HALF * rows
    total = TILES * group
    near = chunks // 2
    diagonal = c == z
    half_x = half_of(c, z)
    for q in range(chunks):
        side, lane = q // near, q % near * LANES
        for s in range(TILES):
            for kind in range(2):
                start = kind * total + s * group
                got = xy_ref[s, kind * chunks + q]
                left[side, start : start + group, lane : lane + LANES] = got
                narrow[kind, q, s * group : (s + 1) * group, :] = got
    acc_x = jnp.zeros((total, LANES), F32)
    acc_y = jnp.zeros((total, LANES), F32)
    kind_x = jnp.where(diagonal, 0, 1)
    for m in range(chunks // 2):
        own = jnp.concatenate([own_ref[2 * m], own_ref[2 * m + 1]], axis=1)
        other = jnp.concatenate([other_ref[2 * m], other_ref[2 * m + 1]], axis=1)
        product = jnp.dot(left[core], own, preferred_element_type=F32)
        product += jnp.dot(left[1 - core], other, preferred_element_type=F32)
        for n in range(2):
            k = (x ^ m) * 2 + (yl ^ n)
            part = product[:, n * LANES : (n + 1) * LANES]
            acc_x += part[:total] * narrow[kind_x, k].astype(F32)
            acc_y += part[total:] * narrow[1, k].astype(F32)
    ones = jnp.ones((8, LANES), F32)
    scale_x = jnp.where(diagonal, 1.0, 2.0)
    for s in range(TILES):
        from_x, from_y = (
            lax.dot_general(
                ones,
                acc[s * group : (s + 1) * group],
                (((1,), (1,)), ((), ())),
                precision=lax.Precision.HIGHEST,
                preferred_element_type=F32,
            )[:1]
            for acc in (acc_x, acc_y)
        )
        from_x = from_x * scale_x
        from_y = jnp.where(diagonal, from_y, 0.0)
        low = lax.rem(half_x + s // HALF, 2) == 0
        out_ref[s] = jnp.concatenate(
            [jnp.where(low, from_x, from_y), jnp.where(low, from_y, from_x)], axis=0
        )


def tile(xy, own, other, rows, chunks):
    total = TILES * HALF * rows
    flops = 2 * 2 * total * (chunks * LANES) ** 2
    return pl.pallas_call(
        functools.partial(tile_kernel, rows, chunks),
        out_shape=jax.ShapeDtypeStruct((TILES, 2, HALF * rows), F32),
        in_specs=[VMEM] * 3,
        out_specs=VMEM,
        scratch_shapes=[
            pltpu.VMEM((2, chunks, total, LANES), BF16),
            pltpu.VMEM((2, 2 * total, chunks // 2 * LANES), BF16),
        ],
        cost_estimate=pl.CostEstimate(flops=flops, bytes_accessed=4_000_000, transcendentals=0),
        compiler_params=pltpu.CompilerParams(vmem_limit_bytes=16 * 1024 * 1024),
        name="tile",
    )(xy, own, other)


def retile(gain):
    core, x, yl = (lax.axis_index(name) for name in ("core", "x", "yl"))
    panel = gain.shape[1]
    halves = gain.reshape(TILES // 4, 2, -1, panel)
    kept = lax.dynamic_index_in_dim(halves, core, 1, keepdims=False)
    given = lax.dynamic_index_in_dim(halves, 1 - core, 1, keepdims=False)
    swap = [(0, 1), (1, 0)]
    taken = lax.ppermute(given, "core", swap)
    first = jnp.where(core == 0, kept, taken)
    second = jnp.where(core == 0, taken, kept)
    blocks = jnp.concatenate([first, second], axis=0)
    got = []
    for m in range(4):
        for n in range(2):
            block = lax.dynamic_index_in_dim(blocks, (x ^ m) * 2 + (yl ^ n), 0, keepdims=False)
            if m or n:
                turn = [
                    (a * 2 + b, (a ^ m) * 2 + (b ^ n)) for a in range(4) for b in range(2)
                ]
                block = lax.ppermute(block, ("x", "yl"), turn)
            got.append(block)
    own = jnp.stack(got)
    return own, lax.ppermute(own, "core", swap)


def shards(jacobian, gain, variance):
    rows, width = jacobian.shape
    chunks = width // TILES // LANES
    parts = jacobian.reshape(rows, TILES, chunks, LANES).transpose(1, 0, 2, 3)
    parts = parts.reshape(TILES, rows * chunks, LANES)
    planes = exchange(pick(parts), "z")
    planes = planes.reshape(TILES, (HALF + 1) * rows * chunks, LANES)
    xy = exchange(spread(planes, rows, chunks), PLANE)
    own, other = retile(gain)
    partial = tile(xy, own, other, rows, chunks)
    in_plane = exchange(partial, PLANE).sum(axis=0)
    in_plane = in_plane.reshape(2, rows, HALF).transpose(0, 2, 1).reshape(TILES, rows)
    return variance - exchange(in_plane, "z").sum(axis=0)


def solution(mesh):
    devices = mesh.devices.reshape(2, 2, TILES, 4, 2)
    return jax.shard_map(
        shards,
        mesh=Mesh(devices, ALL),
        in_specs=(P(ALL, None), P(("yh", "core"), ("z", "x", "yl")), P(ALL)),
        out_specs=P(ALL),
        check_vma=False,
    )
```

time: 515 us -> 129 us (0.25)
  waiting for transfers between devices: 218 us -> 20.4 us
  blocking collectives: 206 us -> 39.1 us
  starting transfers between devices: 19.1 us -> 55 us
  local copies, waits for them, and re-layouts: 36.6 us -> 3.59 us
  between operations: 13.2 us -> 0.29 us
  other arithmetic: 12.8 us -> 2.89 us
  matrix products: 8.9 us -> 0 us
  Pallas kernels: 0 us -> 5.89 us
    all_gather x5 -> x0, waiting for transfers between devices: 210 us -> none  [gather_in_order(): parts = lax.all_gather(parts, axes[k], axis=0, tiled=True)]
    unnamed x1 -> x0, blocking collectives: 110 us -> none
    all_gather x4 -> x0, blocking collectives: 54 us -> none  [gather_in_order(): parts = lax.all_gather(parts, axes[k], axis=0, tiled=True)]
    reshape x6 -> x2, local copies, waits for them, and re-layouts: 34.5 us -> 1.09 us  [the longest x1 1.01 us: shards(): parts = parts.reshape(TILES, rows * chunks, LANES)]
    ppermute x0 -> x9, starting transfers between devices: none -> 32.5 us  [the longest x7 22.3 us: retile(): block = lax.ppermute(block, ('x', 'yl'), turn)]
    concatenate x1 -> x0, other arithmetic: 12.1 us -> none  [gather_all_axes(): return in_order(jnp.concatenate(gathered, axis=cut + 1), dim)]
    ppermute x0 -> x9, waiting for transfers between devices: none -> 9.83 us  [the longest x7 5.96 us: retile(): block = lax.ppermute(block, ('x', 'yl'), turn)]
    dot_general x1 -> x0, matrix products: 8.9 us -> none  [shards(): jnp.dot(gathered, gain_inverse, preferred_element_type=jnp.float32)]
  transfers between devices with their start and end apart: 6 -> 11, of which waited for: 5 -> 7; matrix products, arithmetic and copies ran while one was open for 3% -> 2% of each run, Pallas kernels for 0% -> 2%
where the time goes in v2:
time: 129 us; the launch traced here: 127 us
  starting transfers between devices  55 us (43%)
  blocking collectives  39.1 us (30%)
  waiting for transfers between devices  20.4 us (16%)
  Pallas kernels  5.89 us (5%)
  local copies, waits for them, and re-layouts  3.59 us (3%)
  other arithmetic  2.89 us (2%)
    all_to_all x2, blocking collectives, exchange(): return lax.all_to_all(parts, axis, split_axis=0, concat_axis=0, tiled=True)  39.1 us
    all_to_all x2, starting transfers between devices, exchange(): return lax.all_to_all(parts, axis, split_axis=0, concat_axis=0, tiled=True)  22.5 us
    ppermute x7, starting transfers between devices, retile(): block = lax.ppermute(block, ('x', 'yl'), turn)  22.3 us
    all_to_all x2, waiting for transfers between devices, exchange(): return lax.all_to_all(parts, axis, split_axis=0, concat_axis=0, tiled=True)  10.6 us
    ppermute x1, starting transfers between devices, retile(): return (own, lax.ppermute(own, 'core', swap))  7.38 us
    ppermute x7, waiting for transfers between devices, retile(): block = lax.ppermute(block, ('x', 'yl'), turn)  5.96 us
    ppermute x1, starting transfers between devices, retile(): taken = lax.ppermute(given, 'core', swap)  2.86 us
    pallas_call x1, Pallas kernels, tile(): pl.pallas_call(functools.partial(tile_kernel, rows, chunks), out_shape=ja...  2.65 us
  transfers between devices with their start and end apart: 11, of which 7 were waited for; matrix products, arithmetic and copies ran while one was open for 2% of the time, Pallas kernels for 2%

profile of v2, /device:TPU:1, one launch (start us, length us, event | category | flops | bytes accessed | tf_op | source)
XLA Modules:
  0.0 127.2 jit_solution(16366273881770016977)
XLA Ops:
  0.0 0.0 copy-start.2
  0.0 1.0 copy_bitcast_fusion.1.in_ref
  1.0 1.2 pick.1
  2.2 15.7 %all-to-all-start = ((bf16[16,9,24,128]{3,2,1,0:T(8,128)(2,1)}), bf16[16,9,24,128]{3,2,1,0:T(8,128)(2,1)S(1)}, u32[]{:S(2)}, u32[]{:S(2)}) async-start(bf16[16,9,24,128]{3,2,1,0:T(8,128)(2,1)} %pick.1), calls=%async_computation | async-start | bytes 1769472 | tf_op jit(solution)/shard_map/all_to_all | solution.py:39
  17.9 0.0 copy-done.2
  18.0 2.9 %collective-permute-start = (bf16[4,512,128]{2,1,0:T(8,128)(2,1)S(1)}, bf16[4,512,128]{2,1,0:T(8,128)(2,1)}, u32[]{:S(2)}, u32[]{:S(2)}) collective-permute-start(bf16[4,512,128]{2,1,0:T(8,128)(2,1)S(1)} %dynamic-slice_bitcast_fusion), channel_id=1, source_target_pairs={{0,128},{128,0},{1,129},{129,1},{2,130},{130,2},{3,131},{131,3},{4... | collective-permute-start | bytes 1572872 | tf_op jit(solution)/shard_map/ppermute | solution.py:178
  20.9 1.6 %collective-permute-done = bf16[4,512,128]{2,1,0:T(8,128)(2,1)} collective-permute-done((bf16[4,512,128]{2,1,0:T(8,128)(2,1)S(1)}, bf16[4,512,128]{2,1,0:T(8,128)(2,1)}, u32[]{:S(2)}, u32[]{:S(2)}) %collective-permute-start) | collective-permute-done | bytes 524320 | tf_op jit(solution)/shard_map/ppermute | solution.py:178
  22.5 1.1 bitcast_select_fusion.1
  23.6 1.1 fusion.15
  24.7 3.2 %collective-permute-start.1 = (bf16[512,128]{1,0:T(8,128)(2,1)}, bf16[512,128]{1,0:T(8,128)(2,1)S(1)}, u32[]{:S(2)}, u32[]{:S(2)}) collective-permute-start(bf16[512,128]{1,0:T(8,128)(2,1)} %get-tuple-element.9), channel_id=1, source_target_pairs={{0,1},{1,0},{2,3},{3,2},{4,5},{5,4},{6,7},{7,6},{8,9},{9,8},{10,11... | collective-permute-start | bytes 393224 | tf_op jit(solution)/shard_map/ppermute | solution.py:190
  27.9 0.0 copy-start.3
  27.9 0.1 fusion.9
  28.0 4.4 %collective-permute-start.6 = (bf16[512,128]{1,0:T(8,128)(2,1)S(1)}, bf16[512,128]{1,0:T(8,128)(2,1)S(1)}, u32[]{:S(2)}, u32[]{:S(2)}) collective-permute-start(bf16[512,128]{1,0:T(8,128)(2,1)S(1)} %get-tuple-element.13), channel_id=1, source_target_pairs={{0,6},{1,7},{2,4},{3,5},{4,2},{5,3},{6,0},{7,1},{8,14},{9,15},{10,... | collective-permute-start | bytes 393224 | tf_op jit(solution)/shard_map/ppermute | solution.py:190
  32.4 2.3 %collective-permute-start.5 = (bf16[512,128]{1,0:T(8,128)(2,1)S(1)}, bf16[512,128]{1,0:T(8,128)(2,1)S(1)}, u32[]{:S(2)}, u32[]{:S(2)}) collective-permute-start(bf16[512,128]{1,0:T(8,128)(2,1)S(1)} %get-tuple-element.14), channel_id=1, source_target_pairs={{0,5},{1,4},{2,7},{3,6},{4,1},{5,0},{6,3},{7,2},{8,13},{9,12},{10,... | collective-permute-start | bytes 393224 | tf_op jit(solution)/shard_map/ppermute | solution.py:190
  34.8 4.7 %collective-permute-start.7 = (bf16[512,128]{1,0:T(8,128)(2,1)S(1)}, bf16[512,128]{1,0:T(8,128)(2,1)S(1)}, u32[]{:S(2)}, u32[]{:S(2)}) collective-permute-start(bf16[512,128]{1,0:T(8,128)(2,1)S(1)} %get-tuple-element.7), channel_id=1, source_target_pairs={{0,7},{1,6},{2,5},{3,4},{4,3},{5,2},{6,1},{7,0},{8,15},{9,14},{10,... | collective-permute-start | bytes 393224 | tf_op jit(solution)/shard_map/ppermute | solution.py:190
  39.5 2.2 %collective-permute-start.2 = (bf16[512,128]{1,0:T(8,128)(2,1)}, bf16[512,128]{1,0:T(8,128)(2,1)S(1)}, u32[]{:S(2)}, u32[]{:S(2)}) collective-permute-start(bf16[512,128]{1,0:T(8,128)(2,1)} %get-tuple-element.10), channel_id=1, source_target_pairs={{0,2},{1,3},{2,0},{3,1},{4,6},{5,7},{6,4},{7,5},{8,10},{9,11},{10,... | collective-permute-start | bytes 393224 | tf_op jit(solution)/shard_map/ppermute | solution.py:190
  41.7 0.0 collective-permute-done.1
  41.7 2.9 %collective-permute-start.3 = (bf16[512,128]{1,0:T(8,128)(2,1)}, bf16[512,128]{1,0:T(8,128)(2,1)S(1)}, u32[]{:S(2)}, u32[]{:S(2)}) collective-permute-start(bf16[512,128]{1,0:T(8,128)(2,1)} %get-tuple-element.11), channel_id=1, source_target_pairs={{0,3},{1,2},{2,1},{3,0},{4,7},{5,6},{6,5},{7,4},{8,11},{9,10},{10,... | collective-permute-start | bytes 393224 | tf_op jit(solution)/shard_map/ppermute | solution.py:190
  44.7 1.0 collective-permute-done.2
  45.7 0.0 copy-done.3
  45.7 2.5 %collective-permute-start.4 = (bf16[512,128]{1,0:T(8,128)(2,1)S(1)}, bf16[512,128]{1,0:T(8,128)(2,1)S(1)}, u32[]{:S(2)}, u32[]{:S(2)}) collective-permute-start(bf16[512,128]{1,0:T(8,128)(2,1)S(1)} %copy-done.3), channel_id=1, source_target_pairs={{0,4},{1,5},{2,6},{3,7},{4,0},{5,1},{6,2},{7,3},{8,12},{9,13},{10,... | collective-permute-start | bytes 393224 | tf_op jit(solution)/shard_map/ppermute | solution.py:190
  48.3 0.7 collective-permute-done.3
  49.0 4.2 %collective-permute-done.4 = bf16[512,128]{1,0:T(8,128)(2,1)S(1)} collective-permute-done((bf16[512,128]{1,0:T(8,128)(2,1)S(1)}, bf16[512,128]{1,0:T(8,128)(2,1)S(1)}, u32[]{:S(2)}, u32[]{:S(2)}) %collective-permute-start.4) | collective-permute-done | bytes 131104 | tf_op jit(solution)/shard_map/ppermute | solution.py:190
  53.3 0.0 collective-permute-done.5
  53.3 2.9 %all-to-all-done = bf16[16,9,24,128]{3,2,1,0:T(8,128)(2,1)S(1)} async-done(((bf16[16,9,24,128]{3,2,1,0:T(8,128)(2,1)}), bf16[16,9,24,128]{3,2,1,0:T(8,128)(2,1)S(1)}, u32[]{:S(2)}, u32[]{:S(2)}) %all-to-all-start) | async-done | bytes 884768 | tf_op jit(solution)/shard_map/all_to_all | solution.py:39
  56.2 2.1 %spread.1 = bf16[16,16,24,128]{3,2,1,0:T(8,128)(2,1)} custom-call(bf16[16,216,128]{2,1,0:T(8,128)(2,1)S(1)} %bitcast.50), custom_call_target="tpu_custom_call" | custom-call | flops 4000000 | bytes 2500000 | tf_op jit(solution)/shard_map/spread/pallas_call | solution.py:88
  58.3 6.8 %all-to-all-start.1 = ((bf16[16,16,24,128]{3,2,1,0:T(8,128)(2,1)}), bf16[16,16,24,128]{3,2,1,0:T(8,128)(2,1)S(1)}, u32[]{:S(2)}, u32[]{:S(2)}) async-start(bf16[16,16,24,128]{3,2,1,0:T(8,128)(2,1)} %spread.1), calls=%async_computation.1 | async-start | bytes 3145728 | tf_op jit(solution)/shard_map/all_to_all | solution.py:39
  65.0 0.0 collective-permute-done.6
  65.1 0.0 collective-permute-done.7
  65.1 0.0 copy-start.4
  65.1 7.4 %collective-permute-start.8 = (bf16[8,512,128]{2,1,0:T(8,128)(2,1)S(1)}, bf16[8,512,128]{2,1,0:T(8,128)(2,1)S(1)}, u32[]{:S(2)}, u32[]{:S(2)}) collective-permute-start(bf16[8,512,128]{2,1,0:T(8,128)(2,1)S(1)} %bitcast_dynamic-update-slice_fusion.own_ref), channel_id=1, source_target_pairs={{0,128},{128,0},{1,129},{129,1},{2,130},{130,2},{3,131},{131,3},{4... | collective-permute-start | bytes 3145736 | tf_op jit(solution)/shard_map/ppermute | solution.py:193
  72.5 2.3 %collective-permute-done.8.other_ref = bf16[8,512,128]{2,1,0:T(8,128)(2,1)S(1)} collective-permute-done((bf16[8,512,128]{2,1,0:T(8,128)(2,1)S(1)}, bf16[8,512,128]{2,1,0:T(8,128)(2,1)S(1)}, u32[]{:S(2)}, u32[]{:S(2)}) %collective-permute-start.8) | collective-permute-done | bytes 1048608 | tf_op jit(solution)/shard_map/ppermute | solution.py:193
  74.8 0.0 copy-start
  74.8 1.0 copy-done
  75.7 7.7 %all-to-all-done.1.xy_ref = bf16[16,16,24,128]{3,2,1,0:T(8,128)(2,1)S(1)} async-done(((bf16[16,16,24,128]{3,2,1,0:T(8,128)(2,1)}), bf16[16,16,24,128]{3,2,1,0:T(8,128)(2,1)S(1)}, u32[]{:S(2)}, u32[]{:S(2)}) %all-to-all-start.1) | async-done | bytes 1572896 | tf_op jit(solution)/shard_map/all_to_all | solution.py:39
  83.5 0.0 copy-start.1
  83.5 1.2 copy-done.1
  84.7 2.7 %tile.1 = f32[16,2,24]{2,1,0:T(2,128)S(1)} custom-call(bf16[16,16,24,128]{3,2,1,0:T(8,128)(2,1)S(1)} %all-to-all-done.1.xy_ref, bf16[8,512,128]{2,1,0:T(8,128)(2,1)S(1)} %bitcast_dynamic-update-slice_fusion.own_ref, bf16[8,512,128]{2,1,0:T(8,128)(2,1)S(1)} %copy-done.1), custom_call_target="tpu_custom_call" | custom-call | flops 1610612736 | bytes 4000000 | tf_op jit(solution)/shard_map/tile/pallas_call | solution.py:156
  87.3 10.6 %all_to_all.24 = f32[16,2,24]{2,1,0:T(2,128)S(1)} all-to-all(f32[16,2,24]{2,1,0:T(2,128)S(1)} %tile.1), channel_id=1, replica_groups=mesh['yh'=2,'core'=2,'z'=16,'x'=4,'yl'=2] {'yh','x','yl'}, dimensions={0} | all-to-all | bytes 6144 | tf_op jit(solution)/shard_map/all_to_all | solution.py:39
  97.9 0.1 reshape.23
  98.0 0.1 copy.17
  98.1 28.6 %all_to_all.25 = f32[16,1,3]{2,1,0:T(1,128)S(1)} all-to-all(f32[16,1,3]{2,1,0:T(1,128)S(1)} %bitcast.54), channel_id=1, replica_groups=mesh['yh'=2,'core'=2,'z'=16,'x'=4,'yl'=2] {'z'}, dimensions={0} | all-to-all | bytes 384 | tf_op jit(solution)/shard_map/all_to_all | solution.py:39
  126.7 0.0 copy-done.4
  126.7 0.5 sub.7
  (10 shorter events, 0.2 us)
Async XLA Ops:
  0.0 17.9 %copy-start.2 = (bf16[4096,128]{1,0:T(8,128)(2,1)S(1)}, bf16[4096,128]{1,0:T(8,128)(2,1)}, u32[]{:S(2)}) copy-start(bf16[4096,128]{1,0:T(8,128)(2,1)} %param.4) | copy-start | bytes 3145732
  2.2 54.0 %all-to-all-start = ((bf16[16,9,24,128]{3,2,1,0:T(8,128)(2,1)}), bf16[16,9,24,128]{3,2,1,0:T(8,128)(2,1)S(1)}, u32[]{:S(2)}, u32[]{:S(2)}) async-start(bf16[16,9,24,128]{3,2,1,0:T(8,128)(2,1)} %pick.1), calls=%async_computation | async-start | bytes 1769472 | tf_op jit(solution)/shard_map/all_to_all | solution.py:39
  18.0 4.5 %collective-permute-start = (bf16[4,512,128]{2,1,0:T(8,128)(2,1)S(1)}, bf16[4,512,128]{2,1,0:T(8,128)(2,1)}, u32[]{:S(2)}, u32[]{:S(2)}) collective-permute-start(bf16[4,512,128]{2,1,0:T(8,128)(2,1)S(1)} %dynamic-slice_bitcast_fusion), channel_id=1, source_target_pairs={{0,128},{128,0},{1,129},{129,1},{2,130},{130,2},{3,131},{131,3},{4... | collective-permute-start | bytes 1572872 | tf_op jit(solution)/shard_map/ppermute | solution.py:178
  24.7 17.0 %collective-permute-start.1 = (bf16[512,128]{1,0:T(8,128)(2,1)}, bf16[512,128]{1,0:T(8,128)(2,1)S(1)}, u32[]{:S(2)}, u32[]{:S(2)}) collective-permute-start(bf16[512,128]{1,0:T(8,128)(2,1)} %get-tuple-element.9), channel_id=1, source_target_pairs={{0,1},{1,0},{2,3},{3,2},{4,5},{5,4},{6,7},{7,6},{8,9},{9,8},{10,11... | collective-permute-start | bytes 393224 | tf_op jit(solution)/shard_map/ppermute | solution.py:190
  27.9 17.8 %copy-start.3 = (bf16[512,128]{1,0:T(8,128)(2,1)S(1)}, bf16[512,128]{1,0:T(8,128)(2,1)}, u32[]{:S(2)}) copy-start(bf16[512,128]{1,0:T(8,128)(2,1)} %get-tuple-element.12) | copy-start | bytes 393220
  28.0 37.0 %collective-permute-start.6 = (bf16[512,128]{1,0:T(8,128)(2,1)S(1)}, bf16[512,128]{1,0:T(8,128)(2,1)S(1)}, u32[]{:S(2)}, u32[]{:S(2)}) collective-permute-start(bf16[512,128]{1,0:T(8,128)(2,1)S(1)} %get-tuple-element.13), channel_id=1, source_target_pairs={{0,6},{1,7},{2,4},{3,5},{4,2},{5,3},{6,0},{7,1},{8,14},{9,15},{10,... | collective-permute-start | bytes 393224 | tf_op jit(solution)/shard_map/ppermute | solution.py:190
  32.4 20.8 %collective-permute-start.5 = (bf16[512,128]{1,0:T(8,128)(2,1)S(1)}, bf16[512,128]{1,0:T(8,128)(2,1)S(1)}, u32[]{:S(2)}, u32[]{:S(2)}) collective-permute-start(bf16[512,128]{1,0:T(8,128)(2,1)S(1)} %get-tuple-element.14), channel_id=1, source_target_pairs={{0,5},{1,4},{2,7},{3,6},{4,1},{5,0},{6,3},{7,2},{8,13},{9,12},{10,... | collective-permute-start | bytes 393224 | tf_op jit(solution)/shard_map/ppermute | solution.py:190
  34.8 30.3 %collective-permute-start.7 = (bf16[512,128]{1,0:T(8,128)(2,1)S(1)}, bf16[512,128]{1,0:T(8,128)(2,1)S(1)}, u32[]{:S(2)}, u32[]{:S(2)}) collective-permute-start(bf16[512,128]{1,0:T(8,128)(2,1)S(1)} %get-tuple-element.7), channel_id=1, source_target_pairs={{0,7},{1,6},{2,5},{3,4},{4,3},{5,2},{6,1},{7,0},{8,15},{9,14},{10,... | collective-permute-start | bytes 393224 | tf_op jit(solution)/shard_map/ppermute | solution.py:190
  39.5 6.2 %collective-permute-start.2 = (bf16[512,128]{1,0:T(8,128)(2,1)}, bf16[512,128]{1,0:T(8,128)(2,1)S(1)}, u32[]{:S(2)}, u32[]{:S(2)}) collective-permute-start(bf16[512,128]{1,0:T(8,128)(2,1)} %get-tuple-element.10), channel_id=1, source_target_pairs={{0,2},{1,3},{2,0},{3,1},{4,6},{5,7},{6,4},{7,5},{8,10},{9,11},{10,... | collective-permute-start | bytes 393224 | tf_op jit(solution)/shard_map/ppermute | solution.py:190
  41.7 7.2 %collective-permute-start.3 = (bf16[512,128]{1,0:T(8,128)(2,1)}, bf16[512,128]{1,0:T(8,128)(2,1)S(1)}, u32[]{:S(2)}, u32[]{:S(2)}) collective-permute-start(bf16[512,128]{1,0:T(8,128)(2,1)} %get-tuple-element.11), channel_id=1, source_target_pairs={{0,3},{1,2},{2,1},{3,0},{4,7},{5,6},{6,5},{7,4},{8,11},{9,10},{10,... | collective-permute-start | bytes 393224 | tf_op jit(solution)/shard_map/ppermute | solution.py:190
  45.7 7.5 %collective-permute-start.4 = (bf16[512,128]{1,0:T(8,128)(2,1)S(1)}, bf16[512,128]{1,0:T(8,128)(2,1)S(1)}, u32[]{:S(2)}, u32[]{:S(2)}) collective-permute-start(bf16[512,128]{1,0:T(8,128)(2,1)S(1)} %copy-done.3), channel_id=1, source_target_pairs={{0,4},{1,5},{2,6},{3,7},{4,0},{5,1},{6,2},{7,3},{8,12},{9,13},{10,... | collective-permute-start | bytes 393224 | tf_op jit(solution)/shard_map/ppermute | solution.py:190
  58.3 25.2 %all-to-all-start.1 = ((bf16[16,16,24,128]{3,2,1,0:T(8,128)(2,1)}), bf16[16,16,24,128]{3,2,1,0:T(8,128)(2,1)S(1)}, u32[]{:S(2)}, u32[]{:S(2)}) async-start(bf16[16,16,24,128]{3,2,1,0:T(8,128)(2,1)} %spread.1), calls=%async_computation.1 | async-start | bytes 3145728 | tf_op jit(solution)/shard_map/all_to_all | solution.py:39
  65.1 61.7 %copy-start.4 = (f32[3]{0:T(128)S(1)}, f32[3]{0:T(128)}, u32[]{:S(2)}) copy-start(f32[3]{0:T(128)} %param.5) | copy-start | bytes 40
  65.1 9.6 %collective-permute-start.8 = (bf16[8,512,128]{2,1,0:T(8,128)(2,1)S(1)}, bf16[8,512,128]{2,1,0:T(8,128)(2,1)S(1)}, u32[]{:S(2)}, u32[]{:S(2)}) collective-permute-start(bf16[8,512,128]{2,1,0:T(8,128)(2,1)S(1)} %bitcast_dynamic-update-slice_fusion.own_ref), channel_id=1, source_target_pairs={{0,128},{128,0},{1,129},{129,1},{2,130},{130,2},{3,131},{131,3},{4... | collective-permute-start | bytes 3145736 | tf_op jit(solution)/shard_map/ppermute | solution.py:193
  74.8 1.0 copy-start
  83.5 1.2 copy-start.1

commit v3 on v2

--- a/solution.py
+++ b/solution.py
@@ -7,6 +7,7 @@
 from jax.experimental.pallas import tpu as pltpu
 from jax.sharding import Mesh
 from jax.sharding import PartitionSpec as P
+
 
 PLANE = ("yh", "x", "yl")
 ALL = ("yh", "core", "z", "x", "yl")
@@ -97,33 +98,30 @@
     )(parts)
 
 
-def tile_kernel(rows, chunks, xy_ref, own_ref, other_ref, out_ref, narrow, left):
+def tile_kernel(rows, chunks, xy_ref, *refs):
+    *column_refs, out_ref, narrow, left = refs
     z = lax.axis_index("z")
     x = lax.axis_index("x")
     yl = lax.axis_index("yl")
-    core = lax.axis_index("core")
     c = plane_index()
     group = HALF * rows
     total = TILES * group
-    near = chunks // 2
     diagonal = c == z
     half_x = half_of(c, z)
     for q in range(chunks):
-        side, lane = q // near, q % near * LANES
+        lane = q * LANES
         for s in range(TILES):
             for kind in range(2):
                 start = kind * total + s * group
                 got = xy_ref[s, kind * chunks + q]
-                left[side, start : start + group, lane : lane + LANES] = got
+                left[start : start + group, lane : lane + LANES] = got
                 narrow[kind, q, s * group : (s + 1) * group, :] = got
     acc_x = jnp.zeros((total, LANES), F32)
     acc_y = jnp.zeros((total, LANES), F32)
     kind_x = jnp.where(diagonal, 0, 1)
     for m in range(chunks // 2):
-        own = jnp.concatenate([own_ref[2 * m], own_ref[2 * m + 1]], axis=1)
-        other = jnp.concatenate([other_ref[2 * m], other_ref[2 * m + 1]], axis=1)
-        product = jnp.dot(left[core], own, preferred_element_type=F32)
-        product += jnp.dot(left[1 - core], other, preferred_element_type=F32)
+        columns = jnp.concatenate([column_refs[2 * m][...], column_refs[2 * m + 1][...]], axis=1)
+        product = jnp.dot(left[...], columns, preferred_element_type=F32)
         for n in range(2):
             k = (x ^ m) * 2 + (yl ^ n)
             part = product[:, n * LANES : (n + 1) * LANES]
@@ -150,47 +148,40 @@
         )
 
 
-def tile(xy, own, other, rows, chunks):
+def tile(xy, columns, rows, chunks):
     total = TILES * HALF * rows
     flops = 2 * 2 * total * (chunks * LANES) ** 2
     return pl.pallas_call(
         functools.partial(tile_kernel, rows, chunks),
         out_shape=jax.ShapeDtypeStruct((TILES, 2, HALF * rows), F32),
-        in_specs=[VMEM] * 3,
+        in_specs=[VMEM] * (1 + len(columns)),
         out_specs=VMEM,
         scratch_shapes=[
             pltpu.VMEM((2, chunks, total, LANES), BF16),
-            pltpu.VMEM((2, 2 * total, chunks // 2 * LANES), BF16),
+            pltpu.VMEM((2 * total, chunks * LANES), BF16),
         ],
         cost_estimate=pl.CostEstimate(flops=flops, bytes_accessed=4_000_000, transcendentals=0),
         compiler_params=pltpu.CompilerParams(vmem_limit_bytes=16 * 1024 * 1024),
         name="tile",
-    )(xy, own, other)
+    )(xy, *columns)
 
 
 def retile(gain):
     core, x, yl = (lax.axis_index(name) for name in ("core", "x", "yl"))
-    panel = gain.shape[1]
-    halves = gain.reshape(TILES // 4, 2, -1, panel)
-    kept = lax.dynamic_index_in_dim(halves, core, 1, keepdims=False)
-    given = lax.dynamic_index_in_dim(halves, 1 - core, 1, keepdims=False)
-    swap = [(0, 1), (1, 0)]
-    taken = lax.ppermute(given, "core", swap)
-    first = jnp.where(core == 0, kept, taken)
-    second = jnp.where(core == 0, taken, kept)
-    blocks = jnp.concatenate([first, second], axis=0)
+    taken = lax.ppermute(gain, "core", [(0, 1), (1, 0)])
+    own, taken = (part.reshape(TILES // 4, -1, gain.shape[1]) for part in (gain, taken))
     got = []
     for m in range(4):
         for n in range(2):
-            block = lax.dynamic_index_in_dim(blocks, (x ^ m) * 2 + (yl ^ n), 0, keepdims=False)
+            to_x, to_y = x ^ m, yl ^ n
+            at = (to_x % 2) * 2 + to_y
+            kept, given = (lax.dynamic_index_in_dim(part, at, 0, keepdims=False) for part in (own, taken))
+            block = jnp.where(to_x // 2 == core, kept, given)
             if m or n:
-                turn = [
-                    (a * 2 + b, (a ^ m) * 2 + (b ^ n)) for a in range(4) for b in range(2)
-                ]
+                turn = [(a * 2 + b, (a ^ m) * 2 + (b ^ n)) for a in range(4) for b in range(2)]
                 block = lax.ppermute(block, ("x", "yl"), turn)
             got.append(block)
-    own = jnp.stack(got)
-    return own, lax.ppermute(own, "core", swap)
+    return got
 
 
 def shards(jacobian, gain, variance):
@@ -199,10 +190,11 @@
     parts = jacobian.reshape(rows, TILES, chunks, LANES).transpose(1, 0, 2, 3)
     parts = parts.reshape(TILES, rows * chunks, LANES)
     planes = exchange(pick(parts), "z")
+    columns = retile(gain)
     planes = planes.reshape(TILES, (HALF + 1) * rows * chunks, LANES)
-    xy = exchange(spread(planes, rows, chunks), PLANE)
-    own, other = retile(gain)
-    partial = tile(xy, own, other, rows, chunks)
+    sent = spread(planes, rows, chunks)
+    xy = exchange(sent, PLANE)
+    partial = tile(xy, columns, rows, chunks)
     in_plane = exchange(partial, PLANE).sum(axis=0)
     in_plane = in_plane.reshape(2, rows, HALF).transpose(0, 2, 1).reshape(TILES, rows)
     return variance - exchange(in_plane, "z").sum(axis=0)

time: 129 us -> 163 us (1.26)
  waiting for transfers between devices: 20.4 us -> 60.4 us
  starting transfers between devices: 55 us -> 47.1 us
  blocking collectives: 39.1 us -> 41.7 us
    all_to_all x2, waiting for transfers between devices: 10.6 us -> 35.4 us  [exchange(): return lax.all_to_all(parts, axis, split_axis=0, concat_axis=0, tiled=True)]
    ppermute x7, waiting for transfers between devices: 5.96 us -> 25 us  [retile(): block = lax.ppermute(block, ('x', 'yl'), turn)]
    ppermute x2 -> x1, starting transfers between devices: 10.2 us -> 2.86 us  [retile(): taken = lax.ppermute(gain, 'core', [(0, 1), (1, 0)])]
    ppermute x2 -> x1, waiting for transfers between devices: 3.87 us -> 0.01 us  [retile(): taken = lax.ppermute(gain, 'core', [(0, 1), (1, 0)])]
    all_to_all x2, blocking collectives: 39.1 us -> 41.7 us  [exchange(): return lax.all_to_all(parts, axis, split_axis=0, concat_axis=0, tiled=True)]
  transfers between devices with their start and end apart: 11 -> 10, of which waited for: 7 -> 4; matrix products, arithmetic and copies ran while one was open for 2% -> 1% of each run, Pallas kernels for 2% -> 1%
where the time goes in v3:
time: 163 us; the launch traced here: 160 us
  waiting for transfers between devices  60.4 us (37%)
  starting transfers between devices  47.1 us (29%)
  blocking collectives  41.7 us (26%)
  Pallas kernels  5.77 us (4%)
  local copies, waits for them, and re-layouts  2.84 us (2%)
  other arithmetic  2.31 us (1%)
    all_to_all x2, blocking collectives, exchange(): return lax.all_to_all(parts, axis, split_axis=0, concat_axis=0, tiled=True)  41.7 us
    all_to_all x2, waiting for transfers between devices, exchange(): return lax.all_to_all(parts, axis, split_axis=0, concat_axis=0, tiled=True)  35.4 us
    ppermute x7, waiting for transfers between devices, retile(): block = lax.ppermute(block, ('x', 'yl'), turn)  25 us
    all_to_all x2, starting transfers between devices, exchange(): return lax.all_to_all(parts, axis, split_axis=0, concat_axis=0, tiled=True)  22.5 us
    ppermute x7, starting transfers between devices, retile(): block = lax.ppermute(block, ('x', 'yl'), turn)  21.8 us
  transfers between devices with their start and end apart: 10, of which 4 were waited for; matrix products, arithmetic and copies ran while one was open for 1% of the time, Pallas kernels for 1%

profile of v3, /device:TPU:1, one launch (start us, length us, event | category | flops | bytes accessed | tf_op | source)
XLA Modules:
  0.0 160.5 jit_solution(10611959435728306956)
XLA Ops:
  0.0 0.0 copy-start.2
  0.0 1.0 copy_bitcast_fusion.1.in_ref
  1.0 1.2 pick.1
  2.2 15.7 %all-to-all-start = ((bf16[16,9,24,128]{3,2,1,0:T(8,128)(2,1)}), bf16[16,9,24,128]{3,2,1,0:T(8,128)(2,1)S(1)}, u32[]{:S(2)}, u32[]{:S(2)}) async-start(bf16[16,9,24,128]{3,2,1,0:T(8,128)(2,1)} %pick.1), calls=%async_computation | async-start | bytes 1769472 | tf_op jit(solution)/shard_map/all_to_all | solution.py:40
  17.9 0.0 copy-done.2
  17.9 2.9 %collective-permute-start = (bf16[4096,128]{1,0:T(8,128)(2,1)S(1)}, bf16[4096,128]{1,0:T(8,128)(2,1)}, u32[]{:S(2)}, u32[]{:S(2)}) collective-permute-start(bf16[4096,128]{1,0:T(8,128)(2,1)S(1)} %copy-done.2), channel_id=1, source_target_pairs={{0,128},{128,0},{1,129},{129,1},{2,130},{130,2},{3,131},{131,3},{4... | collective-permute-start | bytes 3145736 | tf_op jit(solution)/shard_map/ppermute | solution.py:171
  20.8 35.4 %all-to-all-done = bf16[16,9,24,128]{3,2,1,0:T(8,128)(2,1)S(1)} async-done(((bf16[16,9,24,128]{3,2,1,0:T(8,128)(2,1)}), bf16[16,9,24,128]{3,2,1,0:T(8,128)(2,1)S(1)}, u32[]{:S(2)}, u32[]{:S(2)}) %all-to-all-start) | async-done | bytes 884768 | tf_op jit(solution)/shard_map/all_to_all | solution.py:40
  56.2 2.1 %spread.1 = bf16[16,16,24,128]{3,2,1,0:T(8,128)(2,1)} custom-call(bf16[16,216,128]{2,1,0:T(8,128)(2,1)S(1)} %bitcast.30), custom_call_target="tpu_custom_call" | custom-call | flops 4000000 | bytes 2500000 | tf_op jit(solution)/shard_map/spread/pallas_call | solution.py:89
  58.3 6.8 %all-to-all-start.1 = ((bf16[16,16,24,128]{3,2,1,0:T(8,128)(2,1)}), bf16[16,16,24,128]{3,2,1,0:T(8,128)(2,1)S(1)}, u32[]{:S(2)}, u32[]{:S(2)}) async-start(bf16[16,16,24,128]{3,2,1,0:T(8,128)(2,1)} %spread.1), calls=%async_computation.1 | async-start | bytes 3145728 | tf_op jit(solution)/shard_map/all_to_all | solution.py:40
  65.2 0.0 collective-permute-done
  65.2 1.7 %select_bitcast_fusion = (bf16[1024,128]{1,0:T(8,128)(2,1)S(1)}, bf16[1024,128]{1,0:T(8,128)(2,1)S(1)}, bf16[1024,128]{1,0:T(8,128)(2,1)S(1)}, bf16[1024,128]{1,...) fusion(bf16[4,1024,128]{2,1,0:T(8,128)(2,1)} %bitcast.4, ...), kind=kLoop, calls=%fused_computation | loop fusion | flops 1048576 | bytes 6291492 | tf_op jit(solution)/shard_map/jit(_where)/select_n | solution.py:179
  67.0 5.2 %collective-permute-start.7 = (bf16[1024,128]{1,0:T(8,128)(2,1)S(1)}, bf16[1024,128]{1,0:T(8,128)(2,1)S(1)}, u32[]{:S(2)}, u32[]{:S(2)}) collective-permute-start(bf16[1024,128]{1,0:T(8,128)(2,1)S(1)} %get-tuple-element.5), channel_id=1, source_target_pairs={{0,7},{1,6},{2,5},{3,4},{4,3},{5,2},{6,1},{7,0},{8,15},{9,14},{10,... | collective-permute-start | bytes 786440 | tf_op jit(solution)/shard_map/ppermute | solution.py:182
  72.2 2.2 %collective-permute-start.6 = (bf16[1024,128]{1,0:T(8,128)(2,1)S(1)}, bf16[1024,128]{1,0:T(8,128)(2,1)S(1)}, u32[]{:S(2)}, u32[]{:S(2)}) collective-permute-start(bf16[1024,128]{1,0:T(8,128)(2,1)S(1)} %get-tuple-element.6), channel_id=1, source_target_pairs={{0,6},{1,7},{2,4},{3,5},{4,2},{5,3},{6,0},{7,1},{8,14},{9,15},{10,... | collective-permute-start | bytes 786440 | tf_op jit(solution)/shard_map/ppermute | solution.py:182
  74.4 3.4 %collective-permute-start.5 = (bf16[1024,128]{1,0:T(8,128)(2,1)S(1)}, bf16[1024,128]{1,0:T(8,128)(2,1)S(1)}, u32[]{:S(2)}, u32[]{:S(2)}) collective-permute-start(bf16[1024,128]{1,0:T(8,128)(2,1)S(1)} %get-tuple-element.7), channel_id=1, source_target_pairs={{0,5},{1,4},{2,7},{3,6},{4,1},{5,0},{6,3},{7,2},{8,13},{9,12},{10,... | collective-permute-start | bytes 786440 | tf_op jit(solution)/shard_map/ppermute | solution.py:182
  77.8 3.4 %collective-permute-start.4 = (bf16[1024,128]{1,0:T(8,128)(2,1)S(1)}, bf16[1024,128]{1,0:T(8,128)(2,1)S(1)}, u32[]{:S(2)}, u32[]{:S(2)}) collective-permute-start(bf16[1024,128]{1,0:T(8,128)(2,1)S(1)} %get-tuple-element.8), channel_id=1, source_target_pairs={{0,4},{1,5},{2,6},{3,7},{4,0},{5,1},{6,2},{7,3},{8,12},{9,13},{10,... | collective-permute-start | bytes 786440 | tf_op jit(solution)/shard_map/ppermute | solution.py:182
  81.2 2.8 %collective-permute-start.3 = (bf16[1024,128]{1,0:T(8,128)(2,1)S(1)}, bf16[1024,128]{1,0:T(8,128)(2,1)S(1)}, u32[]{:S(2)}, u32[]{:S(2)}) collective-permute-start(bf16[1024,128]{1,0:T(8,128)(2,1)S(1)} %get-tuple-element.9), channel_id=1, source_target_pairs={{0,3},{1,2},{2,1},{3,0},{4,7},{5,6},{6,5},{7,4},{8,11},{9,10},{10,... | collective-permute-start | bytes 786440 | tf_op jit(solution)/shard_map/ppermute | solution.py:182
  84.0 15.9 %collective-permute-done.7.refs_7_ = bf16[1024,128]{1,0:T(8,128)(2,1)S(1)} collective-permute-done((bf16[1024,128]{1,0:T(8,128)(2,1)S(1)}, bf16[1024,128]{1,0:T(8,128)(2,1)S(1)}, u32[]{:S(2)}, u32[]{:S(2)}) %collective-permute-start.7) | collective-permute-done | bytes 262176 | tf_op jit(solution)/shard_map/ppermute | solution.py:182
  99.9 1.9 %collective-permute-start.2 = (bf16[1024,128]{1,0:T(8,128)(2,1)S(1)}, bf16[1024,128]{1,0:T(8,128)(2,1)S(1)}, u32[]{:S(2)}, u32[]{:S(2)}) collective-permute-start(bf16[1024,128]{1,0:T(8,128)(2,1)S(1)} %get-tuple-element.10), channel_id=1, source_target_pairs={{0,2},{1,3},{2,0},{3,1},{4,6},{5,7},{6,4},{7,5},{8,10},{9,11},{10,... | collective-permute-start | bytes 786440 | tf_op jit(solution)/shard_map/ppermute | solution.py:182
  101.8 4.6 %collective-permute-done.6.refs_6_ = bf16[1024,128]{1,0:T(8,128)(2,1)S(1)} collective-permute-done((bf16[1024,128]{1,0:T(8,128)(2,1)S(1)}, bf16[1024,128]{1,0:T(8,128)(2,1)S(1)}, u32[]{:S(2)}, u32[]{:S(2)}) %collective-permute-start.6) | collective-permute-done | bytes 262176 | tf_op jit(solution)/shard_map/ppermute | solution.py:182
  106.4 2.8 %collective-permute-start.1 = (bf16[1024,128]{1,0:T(8,128)(2,1)S(1)}, bf16[1024,128]{1,0:T(8,128)(2,1)S(1)}, u32[]{:S(2)}, u32[]{:S(2)}) collective-permute-start(bf16[1024,128]{1,0:T(8,128)(2,1)S(1)} %get-tuple-element.11), channel_id=1, source_target_pairs={{0,1},{1,0},{2,3},{3,2},{4,5},{5,4},{6,7},{7,6},{8,9},{9,8},{10,11... | collective-permute-start | bytes 786440 | tf_op jit(solution)/shard_map/ppermute | solution.py:182
  109.3 0.0 collective-permute-done.5.refs_5_
  109.3 0.0 collective-permute-done.4.refs_4_
  109.3 0.0 collective-permute-done.3.refs_3_
  109.3 0.0 collective-permute-done.2.refs_2_
  109.3 4.5 %collective-permute-done.1.refs_1_ = bf16[1024,128]{1,0:T(8,128)(2,1)S(1)} collective-permute-done((bf16[1024,128]{1,0:T(8,128)(2,1)S(1)}, bf16[1024,128]{1,0:T(8,128)(2,1)S(1)}, u32[]{:S(2)}, u32[]{:S(2)}) %collective-permute-start.1) | collective-permute-done | bytes 262176 | tf_op jit(solution)/shard_map/ppermute | solution.py:182
  113.8 0.0 copy-start
  113.8 0.7 copy-done
  114.5 0.0 all-to-all-done.1.xy_ref
  114.5 0.0 copy-start.1
  114.5 0.9 copy-done.1
  115.5 0.0 copy-start.3
  115.5 2.5 %tile.1 = f32[16,2,24]{2,1,0:T(2,128)S(1)} custom-call(bf16[16,16,24,128]{3,2,1,0:T(8,128)(2,1)S(1)} %all-to-all-done.1.xy_ref, bf16[1024,128]{1,0:T(8,128)(2,1)S(1)} %get-tuple-element.12.refs_0_, bf16[1024,128]{1,0:T(8,128)(2,1)S(1)} %copy-done.1, bf16[1024,128]{1,0:T(8,128)(2,1)S(1)} %collective-permute-done.2.refs_2_, ...), custom_call_target="tpu_custom_call" | custom-call | flops 1610612736 | bytes 4000000 | tf_op jit(solution)/shard_map/tile/pallas_call | solution.py:154
  118.0 11.2 %all_to_all.24 = f32[16,2,24]{2,1,0:T(2,128)S(1)} all-to-all(f32[16,2,24]{2,1,0:T(2,128)S(1)} %tile.1), channel_id=1, replica_groups=mesh['yh'=2,'core'=2,'z'=16,'x'=4,'yl'=2] {'yh','x','yl'}, dimensions={0} | all-to-all | bytes 6144 | tf_op jit(solution)/shard_map/all_to_all | solution.py:40
  129.3 0.1 reshape.43
  129.3 0.1 copy.11
  129.4 30.5 %all_to_all.25 = f32[16,1,3]{2,1,0:T(1,128)S(1)} all-to-all(f32[16,1,3]{2,1,0:T(1,128)S(1)} %bitcast.33), channel_id=1, replica_groups=mesh['yh'=2,'core'=2,'z'=16,'x'=4,'yl'=2] {'z'}, dimensions={0} | all-to-all | bytes 384 | tf_op jit(solution)/shard_map/all_to_all | solution.py:40
  160.0 0.0 copy-done.3
  160.0 0.5 sub.24
  (2 shorter events, 0.1 us)
Async XLA Ops:
  0.0 17.9 %copy-start.2 = (bf16[4096,128]{1,0:T(8,128)(2,1)S(1)}, bf16[4096,128]{1,0:T(8,128)(2,1)}, u32[]{:S(2)}) copy-start(bf16[4096,128]{1,0:T(8,128)(2,1)} %param.4) | copy-start | bytes 3145732
  2.2 54.0 %all-to-all-start = ((bf16[16,9,24,128]{3,2,1,0:T(8,128)(2,1)}), bf16[16,9,24,128]{3,2,1,0:T(8,128)(2,1)S(1)}, u32[]{:S(2)}, u32[]{:S(2)}) async-start(bf16[16,9,24,128]{3,2,1,0:T(8,128)(2,1)} %pick.1), calls=%async_computation | async-start | bytes 1769472 | tf_op jit(solution)/shard_map/all_to_all | solution.py:40
  17.9 47.3 %collective-permute-start = (bf16[4096,128]{1,0:T(8,128)(2,1)S(1)}, bf16[4096,128]{1,0:T(8,128)(2,1)}, u32[]{:S(2)}, u32[]{:S(2)}) collective-permute-start(bf16[4096,128]{1,0:T(8,128)(2,1)S(1)} %copy-done.2), channel_id=1, source_target_pairs={{0,128},{128,0},{1,129},{129,1},{2,130},{130,2},{3,131},{131,3},{4... | collective-permute-start | bytes 3145736 | tf_op jit(solution)/shard_map/ppermute | solution.py:171
  58.3 56.3 %all-to-all-start.1 = ((bf16[16,16,24,128]{3,2,1,0:T(8,128)(2,1)}), bf16[16,16,24,128]{3,2,1,0:T(8,128)(2,1)S(1)}, u32[]{:S(2)}, u32[]{:S(2)}) async-start(bf16[16,16,24,128]{3,2,1,0:T(8,128)(2,1)} %spread.1), calls=%async_computation.1 | async-start | bytes 3145728 | tf_op jit(solution)/shard_map/all_to_all | solution.py:40
  67.0 32.9 %collective-permute-start.7 = (bf16[1024,128]{1,0:T(8,128)(2,1)S(1)}, bf16[1024,128]{1,0:T(8,128)(2,1)S(1)}, u32[]{:S(2)}, u32[]{:S(2)}) collective-permute-start(bf16[1024,128]{1,0:T(8,128)(2,1)S(1)} %get-tuple-element.5), channel_id=1, source_target_pairs={{0,7},{1,6},{2,5},{3,4},{4,3},{5,2},{6,1},{7,0},{8,15},{9,14},{10,... | collective-permute-start | bytes 786440 | tf_op jit(solution)/shard_map/ppermute | solution.py:182
  72.2 34.3 %collective-permute-start.6 = (bf16[1024,128]{1,0:T(8,128)(2,1)S(1)}, bf16[1024,128]{1,0:T(8,128)(2,1)S(1)}, u32[]{:S(2)}, u32[]{:S(2)}) collective-permute-start(bf16[1024,128]{1,0:T(8,128)(2,1)S(1)} %get-tuple-element.6), channel_id=1, source_target_pairs={{0,6},{1,7},{2,4},{3,5},{4,2},{5,3},{6,0},{7,1},{8,14},{9,15},{10,... | collective-permute-start | bytes 786440 | tf_op jit(solution)/shard_map/ppermute | solution.py:182
  74.4 34.9 %collective-permute-start.5 = (bf16[1024,128]{1,0:T(8,128)(2,1)S(1)}, bf16[1024,128]{1,0:T(8,128)(2,1)S(1)}, u32[]{:S(2)}, u32[]{:S(2)}) collective-permute-start(bf16[1024,128]{1,0:T(8,128)(2,1)S(1)} %get-tuple-element.7), channel_id=1, source_target_pairs={{0,5},{1,4},{2,7},{3,6},{4,1},{5,0},{6,3},{7,2},{8,13},{9,12},{10,... | collective-permute-start | bytes 786440 | tf_op jit(solution)/shard_map/ppermute | solution.py:182
  77.8 31.5 %collective-permute-start.4 = (bf16[1024,128]{1,0:T(8,128)(2,1)S(1)}, bf16[1024,128]{1,0:T(8,128)(2,1)S(1)}, u32[]{:S(2)}, u32[]{:S(2)}) collective-permute-start(bf16[1024,128]{1,0:T(8,128)(2,1)S(1)} %get-tuple-element.8), channel_id=1, source_target_pairs={{0,4},{1,5},{2,6},{3,7},{4,0},{5,1},{6,2},{7,3},{8,12},{9,13},{10,... | collective-permute-start | bytes 786440 | tf_op jit(solution)/shard_map/ppermute | solution.py:182
  81.2 28.1 %collective-permute-start.3 = (bf16[1024,128]{1,0:T(8,128)(2,1)S(1)}, bf16[1024,128]{1,0:T(8,128)(2,1)S(1)}, u32[]{:S(2)}, u32[]{:S(2)}) collective-permute-start(bf16[1024,128]{1,0:T(8,128)(2,1)S(1)} %get-tuple-element.9), channel_id=1, source_target_pairs={{0,3},{1,2},{2,1},{3,0},{4,7},{5,6},{6,5},{7,4},{8,11},{9,10},{10,... | collective-permute-start | bytes 786440 | tf_op jit(solution)/shard_map/ppermute | solution.py:182
  99.9 9.4 %collective-permute-start.2 = (bf16[1024,128]{1,0:T(8,128)(2,1)S(1)}, bf16[1024,128]{1,0:T(8,128)(2,1)S(1)}, u32[]{:S(2)}, u32[]{:S(2)}) collective-permute-start(bf16[1024,128]{1,0:T(8,128)(2,1)S(1)} %get-tuple-element.10), channel_id=1, source_target_pairs={{0,2},{1,3},{2,0},{3,1},{4,6},{5,7},{6,4},{7,5},{8,10},{9,11},{10,... | collective-permute-start | bytes 786440 | tf_op jit(solution)/shard_map/ppermute | solution.py:182
  106.4 7.4 %collective-permute-start.1 = (bf16[1024,128]{1,0:T(8,128)(2,1)S(1)}, bf16[1024,128]{1,0:T(8,128)(2,1)S(1)}, u32[]{:S(2)}, u32[]{:S(2)}) collective-permute-start(bf16[1024,128]{1,0:T(8,128)(2,1)S(1)} %get-tuple-element.11), channel_id=1, source_target_pairs={{0,1},{1,0},{2,3},{3,2},{4,5},{5,4},{6,7},{7,6},{8,9},{9,8},{10,11... | collective-permute-start | bytes 786440 | tf_op jit(solution)/shard_map/ppermute | solution.py:182
  113.8 0.7 copy-start
  114.5 1.0 copy-start.1
  115.5 44.5 %copy-start.3 = (f32[3]{0:T(128)S(1)}, f32[3]{0:T(128)}, u32[]{:S(2)}) copy-start(f32[3]{0:T(128)} %param.5) | copy-start | bytes 40

commit v4 on v3

v4 whole, which is shorter than its diff:
```python
import functools
import itertools

import jax
import jax.numpy as jnp
from jax import lax
from jax.experimental import pallas as pl
from jax.experimental.pallas import tpu as pltpu
from jax.sharding import Mesh
from jax.sharding import PartitionSpec as P


PLANE = ("yh", "x", "yl")
ALL = ("yh", "core", "z", "x", "yl")
F32 = jnp.float32
BF16 = jnp.bfloat16
TILES = 16
HALF = TILES // 2
QUAD = 4
FAR = 7
NEAR = 8
LANES = 128
VMEM = pl.BlockSpec(memory_space=pltpu.VMEM)


def plane_index():
    return (lax.axis_index("yh") * 4 + lax.axis_index("x")) * 2 + lax.axis_index("yl")


def half_of(c, z):
    apart = jnp.where(c // QUAD < z // QUAD, 1, 0) ^ (c & 1) ^ (z & 1)
    turn = (z - c) & 3
    beside = jnp.where(turn == 2, 1 ^ ((z >> 1) & 1), turn >> 1)
    return jnp.where(c // QUAD == z // QUAD, beside, apart)


def block_for(z, half, quad, second):
    beside = z ^ 2 if second else (z // QUAD) * QUAD + ((z + 2 * half - 1) & 3)
    apart = QUAD * quad + 2 * second + (half ^ jnp.where(quad < z // QUAD, 1, 0) ^ (z & 1))
    return jnp.where(quad == z // QUAD, beside, apart)


def exchange(parts, axis):
    return lax.all_to_all(parts, axis, split_axis=0, concat_axis=0, tiled=True)


def pick_kernel(in_ref, far_ref, near_ref):
    mine = lax.axis_index("z")
    half = lax.axis_index("yh") ^ (mine & 1)
    for z in range(TILES):
        for slot in range(FAR - 1):
            quad = slot // 2 + jnp.where(slot // 2 >= mine // QUAD, 1, 0)
            far_ref[z, slot] = in_ref[block_for(z, half, quad, slot % 2)]
        far_ref[z, FAR - 1] = in_ref[z]
    for m in range(QUAD):
        z = mine ^ m
        for slot in range(NEAR):
            quad = slot // 2 + jnp.where(slot // 2 >= mine // QUAD, 1, 0)
            if slot < FAR - 1:
                near_ref[m, slot] = in_ref[block_for(z, 1 - half, quad, slot % 2)]
            else:
                near_ref[m, slot] = in_ref[block_for(z, half, mine // QUAD, slot % 2)]


def pick(parts):
    return pl.pallas_call(
        pick_kernel,
        out_shape=(
            jax.ShapeDtypeStruct((TILES, FAR, *parts.shape[1:]), BF16),
            jax.ShapeDtypeStruct((QUAD, NEAR, *parts.shape[1:]), BF16),
        ),
        in_specs=[VMEM],
        out_specs=(VMEM, VMEM),
        cost_estimate=pl.CostEstimate(flops=1_000_000, bytes_accessed=900_000, transcendentals=0),
        compiler_params=pltpu.CompilerParams(vmem_limit_bytes=4 * 1024 * 1024),
        name="pick",
    )(parts)


def spread_kernel(rows, chunks, far_ref, *refs):
    *near_refs, out_ref, wide, stage = refs
    z = lax.axis_index("z")
    top = lax.axis_index("yh")
    block = rows * chunks
    step = FAR * block
    near_at = TILES * step
    for s in range(TILES):
        wide[s * step : (s + 1) * step, :] = far_ref[s].astype(F32)
    for m in range(QUAD):
        at = near_at + m * NEAR * block
        wide[at : at + NEAR * block, :] = near_refs[m][...].astype(F32)

    @pl.loop(0, TILES)
    def _(to):
        diagonal = to == z
        quad = to // QUAD
        beside = quad == z // QUAD
        half_x = jnp.where(diagonal, 0, half_of(to, z))
        half_y = jnp.where(diagonal, 1, half_x)
        second = jnp.where(beside, jnp.where(((z - to) & 3) == 2, 1, 0), (to >> 1) & 1)
        for k in range(HALF):
            swapped = quad == k // 2
            for side, half in ((0, half_x), (1, half_y)):
                parity = half ^ top
                s = 2 * k + parity
                near_s = (z // QUAD) * QUAD + 2 * (k % 2) + jnp.where(beside, parity, 1 - parity)
                last = FAR - 1
                if side == 0:
                    slot = 2 * (quad - jnp.where(quad > k // 2, 1, 0)) + second
                    far = s * FAR + jnp.where(diagonal, last, slot)
                    near_slot = 2 * (quad - jnp.where(quad > z // QUAD, 1, 0)) + second
                    near_slot = jnp.where(beside, last + second, near_slot)
                    near = TILES * FAR + (near_s ^ z) * NEAR + near_slot
                    use_near = jnp.logical_and(swapped, jnp.logical_not(diagonal))
                else:
                    far = s * FAR + last
                    near = near_s * FAR + last
                    use_near = jnp.logical_and(swapped, jnp.logical_not(beside))
                at = pl.multiple_of(jnp.where(use_near, near, far) * block, HALF)
                stage[side, k * block : (k + 1) * block, :] = wide[pl.ds(at, block), :]
        for side in range(2):
            for q in range(chunks):
                got = [
                    stage[side, pl.ds(r * chunks + q, HALF, stride=block), :] for r in range(rows)
                ]
                out_ref[to, side * chunks + q] = jnp.concatenate(got, axis=0).astype(BF16)


def spread(far, near, rows, chunks):
    block = rows * chunks
    return pl.pallas_call(
        functools.partial(spread_kernel, rows, chunks),
        out_shape=jax.ShapeDtypeStruct((TILES, 2 * chunks, HALF * rows, LANES), BF16),
        in_specs=[VMEM] * (1 + len(near)),
        out_specs=VMEM,
        scratch_shapes=[
            pltpu.VMEM(((TILES * FAR + QUAD * NEAR) * block, LANES), F32),
            pltpu.VMEM((2, HALF * block, LANES), F32),
        ],
        cost_estimate=pl.CostEstimate(flops=4_000_000, bytes_accessed=2_500_000, transcendentals=0),
        compiler_params=pltpu.CompilerParams(vmem_limit_bytes=8 * 1024 * 1024),
        name="spread",
    )(far, *near)


def tile_kernel(rows, chunks, xy_ref, *refs):
    *column_refs, out_ref, narrow, left = refs
    z = lax.axis_index("z")
    x = lax.axis_index("x")
    yl = lax.axis_index("yl")
    core = lax.axis_index("core")
    c = plane_index()
    group = HALF * rows
    total = TILES * group
    diagonal = c == z
    half_x = jnp.where(diagonal, 0, half_of(c, z))
    half_y = jnp.where(diagonal, 1, half_x)
    beside = c // QUAD == z // QUAD
    for q in range(chunks):
        lane = q * LANES
        for s in range(TILES):
            for kind in range(2):
                start = kind * total + s * group
                got = xy_ref[s, kind * chunks + q]
                left[start : start + group, lane : lane + LANES] = got
                narrow[kind, q, s * group : (s + 1) * group, :] = got
    acc_x = jnp.zeros((total, LANES), F32)
    acc_y = jnp.zeros((total, LANES), F32)
    kind_x = jnp.where(diagonal, 0, 1)
    for m in range(chunks // 2):
        columns = jnp.concatenate([column_refs[2 * m][...], column_refs[2 * m + 1][...]], axis=1)
        product = jnp.dot(left[...], columns, preferred_element_type=F32)
        for n in range(2):
            k = ((core ^ (m // 2)) * 2 + ((x & 1) ^ (m % 2))) * 2 + (yl ^ n)
            part = product[:, n * LANES : (n + 1) * LANES]
            acc_x += part[:total] * narrow[kind_x, k].astype(F32)
            acc_y += part[total:] * narrow[1, k].astype(F32)
    ones = jnp.ones((LANES, LANES), F32)
    sum_x, sum_y = (
        jnp.dot(acc, ones, precision=lax.Precision.HIGHEST, preferred_element_type=F32)
        for acc in (acc_x, acc_y)
    )
    lane = lax.broadcasted_iota(jnp.int32, (group, LANES), 1)
    row = lax.broadcasted_iota(jnp.int32, (group, LANES), 0)
    r, k = row // HALF, row % HALF
    scale_x = jnp.where(diagonal, 1.0, 2.0)
    for top in range(2):
        parity = half_x ^ top
        swapped = jnp.logical_and(k // 2 == c // QUAD, jnp.logical_not(beside))
        plane = jnp.where(swapped, (z // QUAD) * QUAD + 2 * (k % 2) + 1 - parity, 2 * k + parity)
        mine_x = lane == r * TILES + plane
        mine_y = jnp.logical_and(lane == r * TILES + 2 * k + (half_y ^ top), diagonal)
        for s in range(top * HALF, (top + 1) * HALF):
            got = jnp.where(mine_x, sum_x[s * group : (s + 1) * group] * scale_x, 0.0)
            got = jnp.where(mine_y, sum_y[s * group : (s + 1) * group], got)
            out_ref[s : s + 1, :] = jnp.sum(got, axis=0, keepdims=True)


def tile(xy, columns, rows, chunks):
    total = TILES * HALF * rows
    flops = 2 * 2 * total * (chunks * LANES) ** 2
    return pl.pallas_call(
        functools.partial(tile_kernel, rows, chunks),
        out_shape=jax.ShapeDtypeStruct((TILES, LANES), F32),
        in_specs=[VMEM] * (1 + len(columns)),
        out_specs=VMEM,
        scratch_shapes=[
            pltpu.VMEM((2, chunks, total, LANES), BF16),
            pltpu.VMEM((2 * total, chunks * LANES), BF16),
        ],
        cost_estimate=pl.CostEstimate(flops=flops, bytes_accessed=4_000_000, transcendentals=0),
        compiler_params=pltpu.CompilerParams(vmem_limit_bytes=16 * 1024 * 1024),
        name="tile",
    )(xy, *columns)


def retile(gain):
    low, yl = lax.axis_index("x") % 2, lax.axis_index("yl")
    blocks = gain.reshape(TILES // 4, -1, gain.shape[1])
    got = []
    for a, b, n in itertools.product(range(2), repeat=3):
        turn = [
            (((s * 2 + h) * 2 + w) * 2 + y, (((h ^ a) * 2 + s) * 2 + (w ^ b)) * 2 + (y ^ n))
            for s, h, w, y in itertools.product(range(2), repeat=4)
        ]
        block = lax.dynamic_index_in_dim(blocks, (low ^ b) * 2 + (yl ^ n), 0, keepdims=False)
        got.append(lax.ppermute(block, ("core", "x", "yl"), turn))
    return got


def shards(jacobian, gain, variance):
    rows, width = jacobian.shape
    chunks = width // TILES // LANES
    parts = jacobian.reshape(rows, TILES, chunks, LANES).transpose(1, 0, 2, 3)
    parts = parts.reshape(TILES, rows * chunks, LANES)
    far, near = pick(parts)
    far = exchange(far, "z").reshape(TILES, FAR * rows * chunks, LANES)
    near = [near[m].reshape(NEAR * rows * chunks, LANES) for m in range(QUAD)]
    for m in range(1, QUAD):
        near[m] = lax.ppermute(near[m], "z", [(s, s ^ m) for s in range(TILES)])
    columns = retile(gain)
    sent = spread(far, near, rows, chunks)
    xy = exchange(sent, PLANE)
    partial = tile(xy, columns, rows, chunks)
    in_plane = exchange(partial, PLANE).sum(axis=0)
    in_plane = in_plane[: rows * TILES].reshape(rows, TILES).transpose(1, 0)
    return variance - exchange(in_plane, "z").sum(axis=0)


def solution(mesh):
    devices = mesh.devices.reshape(2, 2, TILES, 4, 2)
    return jax.shard_map(
        shards,
        mesh=Mesh(devices, ALL),
        in_specs=(P(ALL, None), P(("yh", "core"), ("z", "x", "yl")), P(ALL)),
        out_specs=P(ALL),
        check_vma=False,
    )
```

time: 163 us -> 152 us (0.933)
  waiting for transfers between devices: 60.4 us -> 39.4 us
  starting transfers between devices: 47.1 us -> 65.2 us
  blocking collectives: 41.7 us -> 34.9 us
  other arithmetic: 2.31 us -> 0.58 us
    all_to_all x2, waiting for transfers between devices: 35.4 us -> 0.01 us  [exchange(): return lax.all_to_all(parts, axis, split_axis=0, concat_axis=0, tiled=True)]
    ppermute x8 -> x11, starting transfers between devices: 24.6 us -> 42.6 us  [the longest x8 33.4 us: retile(): got.append(lax.ppermute(block, ('core', 'x', 'yl'), turn))]
    ppermute x8 -> x11, waiting for transfers between devices: 25 us -> 39.4 us  [the longest x3 25.4 us: shards(): near[m] = lax.ppermute(near[m], 'z', [(s, s ^ m) for s in range(TILES)])]
    all_to_all x2, blocking collectives: 41.7 us -> 34.9 us  [exchange(): return lax.all_to_all(parts, axis, split_axis=0, concat_axis=0, tiled=True)]
    select_n x1 -> x0, other arithmetic: 1.74 us -> none  [retile(): block = jnp.where(to_x // 2 == core, kept, given)]
  transfers between devices with their start and end apart: 10 -> 13, of which waited for: 4 -> 9; matrix products, arithmetic and copies ran while one was open for 1% -> 0% of each run, Pallas kernels for 1% -> 0%
where the time goes in v4:
time: 152 us; the launch traced here: 149 us
  starting transfers between devices  65.2 us (43%)
  waiting for transfers between devices  39.4 us (26%)
  blocking collectives  34.9 us (23%)
  Pallas kernels  6.1 us (4%)
  local copies, waits for them, and re-layouts  2.86 us (2%)
    all_to_all x2, blocking collectives, exchange(): return lax.all_to_all(parts, axis, split_axis=0, concat_axis=0, tiled=True)  34.9 us
    ppermute x8, starting transfers between devices, retile(): got.append(lax.ppermute(block, ('core', 'x', 'yl'), turn))  33.4 us
    ppermute x3, waiting for transfers between devices, shards(): near[m] = lax.ppermute(near[m], 'z', [(s, s ^ m) for s in range(TILES)])  25.4 us
    all_to_all x2, starting transfers between devices, exchange(): return lax.all_to_all(parts, axis, split_axis=0, concat_axis=0, tiled=True)  22.6 us
    ppermute x8, waiting for transfers between devices, retile(): got.append(lax.ppermute(block, ('core', 'x', 'yl'), turn))  14 us
    ppermute x3, starting transfers between devices, shards(): near[m] = lax.ppermute(near[m], 'z', [(s, s ^ m) for s in range(TILES)])  9.18 us
  transfers between devices with their start and end apart: 13, of which 9 were waited for; matrix products, arithmetic and copies ran while one was open for 0% of the time, Pallas kernels for 0%

profile of v4, /device:TPU:1, one launch (start us, length us, event | category | flops | bytes accessed | tf_op | source)
XLA Modules:
  0.0 149.2 jit_solution(94754345337183623)
XLA Ops:
  0.0 0.9 copy_bitcast_fusion.1.in_ref
  0.9 1.1 pick.1
  2.0 15.7 %all-to-all-start = ((bf16[16,7,24,128]{3,2,1,0:T(8,128)(2,1)}), bf16[16,7,24,128]{3,2,1,0:T(8,128)(2,1)S(1)}, u32[]{:S(2)}, u32[]{:S(2)}) async-start(bf16[16,7,24,128]{3,2,1,0:T(8,128)(2,1)} %get-tuple-element.7), calls=%async_computation | async-start | bytes 1376256 | tf_op jit(solution)/shard_map/all_to_all | solution.py:44
  17.8 4.2 %collective-permute-start.1 = (bf16[192,128]{1,0:T(8,128)(2,1)S(1)}, bf16[192,128]{1,0:T(8,128)(2,1)S(1)}, u32[]{:S(2)}, u32[]{:S(2)}) collective-permute-start(bf16[192,128]{1,0:T(8,128)(2,1)S(1)} %bitcast.37), channel_id=1, source_target_pairs={{0,16},{8,24},{16,0},{24,8},{32,48},{40,56},{48,32},{56,40},{64,80... | collective-permute-start | bytes 147464 | tf_op jit(solution)/shard_map/ppermute | solution.py:240
  22.0 3.1 %collective-permute-start.2 = (bf16[192,128]{1,0:T(8,128)(2,1)S(1)}, bf16[192,128]{1,0:T(8,128)(2,1)S(1)}, u32[]{:S(2)}, u32[]{:S(2)}) collective-permute-start(bf16[192,128]{1,0:T(8,128)(2,1)S(1)} %bitcast.36), channel_id=1, source_target_pairs={{0,24},{8,16},{16,8},{24,0},{32,56},{40,48},{48,40},{56,32},{64,88... | collective-permute-start | bytes 147464 | tf_op jit(solution)/shard_map/ppermute | solution.py:240
  25.1 1.9 %collective-permute-start = (bf16[192,128]{1,0:T(8,128)(2,1)S(1)}, bf16[192,128]{1,0:T(8,128)(2,1)S(1)}, u32[]{:S(2)}, u32[]{:S(2)}) collective-permute-start(bf16[192,128]{1,0:T(8,128)(2,1)S(1)} %bitcast.35), channel_id=1, source_target_pairs={{0,8},{8,0},{16,24},{24,16},{32,40},{40,32},{48,56},{56,48},{64,72... | collective-permute-start | bytes 147464 | tf_op jit(solution)/shard_map/ppermute | solution.py:240
  27.0 24.5 %collective-permute-done.1.refs_2_ = bf16[192,128]{1,0:T(8,128)(2,1)S(1)} collective-permute-done((bf16[192,128]{1,0:T(8,128)(2,1)S(1)}, bf16[192,128]{1,0:T(8,128)(2,1)S(1)}, u32[]{:S(2)}, u32[]{:S(2)}) %collective-permute-start.1) | collective-permute-done | bytes 49184 | tf_op jit(solution)/shard_map/ppermute | solution.py:240
  51.5 0.9 collective-permute-done.2.refs_3_
  52.4 0.0 collective-permute-done.refs_1_
  52.4 0.0 all-to-all-done
  52.4 2.8 %spread.1 = bf16[16,16,24,128]{3,2,1,0:T(8,128)(2,1)} custom-call(bf16[16,168,128]{2,1,0:T(8,128)(2,1)S(1)} %bitcast.30, bf16[192,128]{1,0:T(8,128)(2,1)S(1)} %bitcast.31, bf16[192,128]{1,0:T(8,128)(2,1)S(1)} %collective-permute-done.refs_1_, bf16[192,128]{1,0:T(8,128)(2,1)S(1)} %collective-permute-done.1.refs_2_, ...), custom_call_target="tpu_custom_call" | custom-call | flops 4000000 | bytes 2500000 | tf_op jit(solution)/shard_map/spread/pallas_call | solution.py:131
  55.2 0.0 copy-start.2
  55.2 6.9 %all-to-all-start.1 = ((bf16[16,16,24,128]{3,2,1,0:T(8,128)(2,1)}), bf16[16,16,24,128]{3,2,1,0:T(8,128)(2,1)S(1)}, u32[]{:S(2)}, u32[]{:S(2)}) async-start(bf16[16,16,24,128]{3,2,1,0:T(8,128)(2,1)} %spread.1), calls=%async_computation.1 | async-start | bytes 3145728 | tf_op jit(solution)/shard_map/all_to_all | solution.py:44
  62.1 0.0 copy-done.2
  62.1 0.1 dynamic-slice_bitcast_fusion
  62.2 5.3 %collective-permute-start.10 = (bf16[1024,128]{1,0:T(8,128)(2,1)S(1)}, bf16[1024,128]{1,0:T(8,128)(2,1)S(1)}, u32[]{:S(2)}, u32[]{:S(2)}) collective-permute-start(bf16[1024,128]{1,0:T(8,128)(2,1)S(1)} %get-tuple-element.9), channel_id=1, source_target_pairs={{0,131},{1,130},{2,129},{3,128},{4,3},{5,2},{6,1},{7,0},{128,135},... | collective-permute-start | bytes 786440 | tf_op jit(solution)/shard_map/ppermute | solution.py:227
  67.6 7.5 %collective-permute-start.6 = (bf16[1024,128]{1,0:T(8,128)(2,1)S(1)}, bf16[1024,128]{1,0:T(8,128)(2,1)S(1)}, u32[]{:S(2)}, u32[]{:S(2)}) collective-permute-start(bf16[1024,128]{1,0:T(8,128)(2,1)S(1)} %get-tuple-element.9), channel_id=1, source_target_pairs={{0,3},{1,2},{2,1},{3,0},{4,131},{5,130},{6,129},{7,128},{128,7},{1... | collective-permute-start | bytes 786440 | tf_op jit(solution)/shard_map/ppermute | solution.py:227
  75.1 3.2 %collective-permute-start.9 = (bf16[1024,128]{1,0:T(8,128)(2,1)S(1)}, bf16[1024,128]{1,0:T(8,128)(2,1)S(1)}, u32[]{:S(2)}, u32[]{:S(2)}) collective-permute-start(bf16[1024,128]{1,0:T(8,128)(2,1)S(1)} %get-tuple-element.10), channel_id=1, source_target_pairs={{0,130},{1,131},{2,128},{3,129},{4,2},{5,3},{6,0},{7,1},{128,134},... | collective-permute-start | bytes 786440 | tf_op jit(solution)/shard_map/ppermute | solution.py:227
  78.4 2.5 %collective-permute-start.5 = (bf16[1024,128]{1,0:T(8,128)(2,1)S(1)}, bf16[1024,128]{1,0:T(8,128)(2,1)S(1)}, u32[]{:S(2)}, u32[]{:S(2)}) collective-permute-start(bf16[1024,128]{1,0:T(8,128)(2,1)S(1)} %get-tuple-element.10), channel_id=1, source_target_pairs={{0,2},{1,3},{2,0},{3,1},{4,130},{5,131},{6,128},{7,129},{128,6},{1... | collective-permute-start | bytes 786440 | tf_op jit(solution)/shard_map/ppermute | solution.py:227
  80.9 3.4 %collective-permute-start.8 = (bf16[1024,128]{1,0:T(8,128)(2,1)S(1)}, bf16[1024,128]{1,0:T(8,128)(2,1)S(1)}, u32[]{:S(2)}, u32[]{:S(2)}) collective-permute-start(bf16[1024,128]{1,0:T(8,128)(2,1)S(1)} %get-tuple-element.11), channel_id=1, source_target_pairs={{0,129},{1,128},{2,131},{3,130},{4,1},{5,0},{6,3},{7,2},{128,133},... | collective-permute-start | bytes 786440 | tf_op jit(solution)/shard_map/ppermute | solution.py:227
  84.3 6.4 %collective-permute-done.10.refs_7_ = bf16[1024,128]{1,0:T(8,128)(2,1)S(1)} collective-permute-done((bf16[1024,128]{1,0:T(8,128)(2,1)S(1)}, bf16[1024,128]{1,0:T(8,128)(2,1)S(1)}, u32[]{:S(2)}, u32[]{:S(2)}) %collective-permute-start.10) | collective-permute-done | bytes 262176 | tf_op jit(solution)/shard_map/ppermute | solution.py:227
  90.7 1.9 %collective-permute-start.4 = (bf16[1024,128]{1,0:T(8,128)(2,1)S(1)}, bf16[1024,128]{1,0:T(8,128)(2,1)S(1)}, u32[]{:S(2)}, u32[]{:S(2)}) collective-permute-start(bf16[1024,128]{1,0:T(8,128)(2,1)S(1)} %get-tuple-element.11), channel_id=1, source_target_pairs={{0,1},{1,0},{2,3},{3,2},{4,129},{5,128},{6,131},{7,130},{128,5},{1... | collective-permute-start | bytes 786440 | tf_op jit(solution)/shard_map/ppermute | solution.py:227
  92.6 0.3 collective-permute-done.6.refs_3_
  93.0 0.0 copy-start.3
  93.0 5.7 %collective-permute-start.7 = (bf16[1024,128]{1,0:T(8,128)(2,1)S(1)}, bf16[1024,128]{1,0:T(8,128)(2,1)S(1)}, u32[]{:S(2)}, u32[]{:S(2)}) collective-permute-start(bf16[1024,128]{1,0:T(8,128)(2,1)S(1)} %get-tuple-element.12), channel_id=1, source_target_pairs={{0,128},{1,129},{2,130},{3,131},{4,0},{5,1},{6,2},{7,3},{128,132},... | collective-permute-start | bytes 786440 | tf_op jit(solution)/shard_map/ppermute | solution.py:227
  98.6 1.2 collective-permute-done.9.refs_6_
  99.9 3.8 %collective-permute-start.3 = (bf16[1024,128]{1,0:T(8,128)(2,1)S(1)}, bf16[1024,128]{1,0:T(8,128)(2,1)S(1)}, u32[]{:S(2)}, u32[]{:S(2)}) collective-permute-start(bf16[1024,128]{1,0:T(8,128)(2,1)S(1)} %get-tuple-element.12), channel_id=1, source_target_pairs={{0,0},{1,1},{2,2},{3,3},{4,128},{5,129},{6,130},{7,131},{128,4},{1... | collective-permute-start | bytes 786440 | tf_op jit(solution)/shard_map/ppermute | solution.py:227
  103.7 0.3 collective-permute-done.5.refs_2_
  104.0 0.0 collective-permute-done.8.refs_5_
  104.0 0.4 collective-permute-done.4.refs_1_
  104.4 0.3 collective-permute-done.7.refs_4_
  104.8 4.9 %collective-permute-done.3.refs_0_ = bf16[1024,128]{1,0:T(8,128)(2,1)S(1)} collective-permute-done((bf16[1024,128]{1,0:T(8,128)(2,1)S(1)}, bf16[1024,128]{1,0:T(8,128)(2,1)S(1)}, u32[]{:S(2)}, u32[]{:S(2)}) %collective-permute-start.3) | collective-permute-done | bytes 262176 | tf_op jit(solution)/shard_map/ppermute | solution.py:227
  109.7 0.0 copy-start
  109.7 0.7 copy-done
  110.4 0.0 all-to-all-done.1.xy_ref
  110.4 0.0 copy-start.1
  110.4 0.9 copy-done.1
  111.3 2.2 %tile.1 = f32[16,128]{1,0:T(8,128)S(1)} custom-call(bf16[16,16,24,128]{3,2,1,0:T(8,128)(2,1)S(1)} %all-to-all-done.1.xy_ref, bf16[1024,128]{1,0:T(8,128)(2,1)S(1)} %copy-done.1, bf16[1024,128]{1,0:T(8,128)(2,1)S(1)} %collective-permute-done.4.refs_1_, bf16[1024,128]{1,0:T(8,128)(2,1)S(1)} %collective-permute-done.5.refs_2_, ...), custom_call_target="tpu_custom_call" | custom-call | flops 1610612736 | bytes 4000000 | tf_op jit(solution)/shard_map/tile/pallas_call | solution.py:202
  113.6 10.2 %all_to_all.28 = f32[16,1,128]{2,1,0:T(1,128)S(1)} all-to-all(f32[16,1,128]{2,1,0:T(1,128)S(1)} %bitcast.32), channel_id=1, replica_groups=mesh['yh'=2,'core'=2,'z'=16,'x'=4,'yl'=2] {'yh','x','yl'}, dimensions={0} | all-to-all | bytes 16384 | tf_op jit(solution)/shard_map/all_to_all | solution.py:44
  123.8 0.1 reshape.31
  123.9 0.1 copy.7
  124.0 24.7 %all_to_all.29 = f32[16,1,3]{2,1,0:T(1,128)S(1)} all-to-all(f32[16,1,3]{2,1,0:T(1,128)S(1)} %copy.7), channel_id=1, replica_groups=mesh['yh'=2,'core'=2,'z'=16,'x'=4,'yl'=2] {'z'}, dimensions={0} | all-to-all | bytes 384 | tf_op jit(solution)/shard_map/all_to_all | solution.py:44
  148.7 0.0 copy-done.3
  148.7 0.5 sub.3
  (3 shorter events, 0.1 us)
Async XLA Ops:
  2.0 50.4 %all-to-all-start = ((bf16[16,7,24,128]{3,2,1,0:T(8,128)(2,1)}), bf16[16,7,24,128]{3,2,1,0:T(8,128)(2,1)S(1)}, u32[]{:S(2)}, u32[]{:S(2)}) async-start(bf16[16,7,24,128]{3,2,1,0:T(8,128)(2,1)} %get-tuple-element.7), calls=%async_computation | async-start | bytes 1376256 | tf_op jit(solution)/shard_map/all_to_all | solution.py:44
  17.8 33.7 %collective-permute-start.1 = (bf16[192,128]{1,0:T(8,128)(2,1)S(1)}, bf16[192,128]{1,0:T(8,128)(2,1)S(1)}, u32[]{:S(2)}, u32[]{:S(2)}) collective-permute-start(bf16[192,128]{1,0:T(8,128)(2,1)S(1)} %bitcast.37), channel_id=1, source_target_pairs={{0,16},{8,24},{16,0},{24,8},{32,48},{40,56},{48,32},{56,40},{64,80... | collective-permute-start | bytes 147464 | tf_op jit(solution)/shard_map/ppermute | solution.py:240
  22.0 30.4 %collective-permute-start.2 = (bf16[192,128]{1,0:T(8,128)(2,1)S(1)}, bf16[192,128]{1,0:T(8,128)(2,1)S(1)}, u32[]{:S(2)}, u32[]{:S(2)}) collective-permute-start(bf16[192,128]{1,0:T(8,128)(2,1)S(1)} %bitcast.36), channel_id=1, source_target_pairs={{0,24},{8,16},{16,8},{24,0},{32,56},{40,48},{48,40},{56,32},{64,88... | collective-permute-start | bytes 147464 | tf_op jit(solution)/shard_map/ppermute | solution.py:240
  25.1 27.3 %collective-permute-start = (bf16[192,128]{1,0:T(8,128)(2,1)S(1)}, bf16[192,128]{1,0:T(8,128)(2,1)S(1)}, u32[]{:S(2)}, u32[]{:S(2)}) collective-permute-start(bf16[192,128]{1,0:T(8,128)(2,1)S(1)} %bitcast.35), channel_id=1, source_target_pairs={{0,8},{8,0},{16,24},{24,16},{32,40},{40,32},{48,56},{56,48},{64,72... | collective-permute-start | bytes 147464 | tf_op jit(solution)/shard_map/ppermute | solution.py:240
  55.2 6.9 %copy-start.2 = (bf16[4096,128]{1,0:T(8,128)(2,1)S(1)}, bf16[4096,128]{1,0:T(8,128)(2,1)}, u32[]{:S(2)}) copy-start(bf16[4096,128]{1,0:T(8,128)(2,1)} %param.4) | copy-start | bytes 3145732
  55.2 55.2 %all-to-all-start.1 = ((bf16[16,16,24,128]{3,2,1,0:T(8,128)(2,1)}), bf16[16,16,24,128]{3,2,1,0:T(8,128)(2,1)S(1)}, u32[]{:S(2)}, u32[]{:S(2)}) async-start(bf16[16,16,24,128]{3,2,1,0:T(8,128)(2,1)} %spread.1), calls=%async_computation.1 | async-start | bytes 3145728 | tf_op jit(solution)/shard_map/all_to_all | solution.py:44
  62.2 28.5 %collective-permute-start.10 = (bf16[1024,128]{1,0:T(8,128)(2,1)S(1)}, bf16[1024,128]{1,0:T(8,128)(2,1)S(1)}, u32[]{:S(2)}, u32[]{:S(2)}) collective-permute-start(bf16[1024,128]{1,0:T(8,128)(2,1)S(1)} %get-tuple-element.9), channel_id=1, source_target_pairs={{0,131},{1,130},{2,129},{3,128},{4,3},{5,2},{6,1},{7,0},{128,135},... | collective-permute-start | bytes 786440 | tf_op jit(solution)/shard_map/ppermute | solution.py:227
  67.6 25.4 %collective-permute-start.6 = (bf16[1024,128]{1,0:T(8,128)(2,1)S(1)}, bf16[1024,128]{1,0:T(8,128)(2,1)S(1)}, u32[]{:S(2)}, u32[]{:S(2)}) collective-permute-start(bf16[1024,128]{1,0:T(8,128)(2,1)S(1)} %get-tuple-element.9), channel_id=1, source_target_pairs={{0,3},{1,2},{2,1},{3,0},{4,131},{5,130},{6,129},{7,128},{128,7},{1... | collective-permute-start | bytes 786440 | tf_op jit(solution)/shard_map/ppermute | solution.py:227
  75.1 24.8 %collective-permute-start.9 = (bf16[1024,128]{1,0:T(8,128)(2,1)S(1)}, bf16[1024,128]{1,0:T(8,128)(2,1)S(1)}, u32[]{:S(2)}, u32[]{:S(2)}) collective-permute-start(bf16[1024,128]{1,0:T(8,128)(2,1)S(1)} %get-tuple-element.10), channel_id=1, source_target_pairs={{0,130},{1,131},{2,128},{3,129},{4,2},{5,3},{6,0},{7,1},{128,134},... | collective-permute-start | bytes 786440 | tf_op jit(solution)/shard_map/ppermute | solution.py:227
  78.4 25.6 %collective-permute-start.5 = (bf16[1024,128]{1,0:T(8,128)(2,1)S(1)}, bf16[1024,128]{1,0:T(8,128)(2,1)S(1)}, u32[]{:S(2)}, u32[]{:S(2)}) collective-permute-start(bf16[1024,128]{1,0:T(8,128)(2,1)S(1)} %get-tuple-element.10), channel_id=1, source_target_pairs={{0,2},{1,3},{2,0},{3,1},{4,130},{5,131},{6,128},{7,129},{128,6},{1... | collective-permute-start | bytes 786440 | tf_op jit(solution)/shard_map/ppermute | solution.py:227
  80.9 23.2 %collective-permute-start.8 = (bf16[1024,128]{1,0:T(8,128)(2,1)S(1)}, bf16[1024,128]{1,0:T(8,128)(2,1)S(1)}, u32[]{:S(2)}, u32[]{:S(2)}) collective-permute-start(bf16[1024,128]{1,0:T(8,128)(2,1)S(1)} %get-tuple-element.11), channel_id=1, source_target_pairs={{0,129},{1,128},{2,131},{3,130},{4,1},{5,0},{6,3},{7,2},{128,133},... | collective-permute-start | bytes 786440 | tf_op jit(solution)/shard_map/ppermute | solution.py:227
  90.7 13.7 %collective-permute-start.4 = (bf16[1024,128]{1,0:T(8,128)(2,1)S(1)}, bf16[1024,128]{1,0:T(8,128)(2,1)S(1)}, u32[]{:S(2)}, u32[]{:S(2)}) collective-permute-start(bf16[1024,128]{1,0:T(8,128)(2,1)S(1)} %get-tuple-element.11), channel_id=1, source_target_pairs={{0,1},{1,0},{2,3},{3,2},{4,129},{5,128},{6,131},{7,130},{128,5},{1... | collective-permute-start | bytes 786440 | tf_op jit(solution)/shard_map/ppermute | solution.py:227
  93.0 55.7 %copy-start.3 = (f32[3]{0:T(128)S(1)}, f32[3]{0:T(128)}, u32[]{:S(2)}) copy-start(f32[3]{0:T(128)} %param.5) | copy-start | bytes 40
  93.0 11.8 %collective-permute-start.7 = (bf16[1024,128]{1,0:T(8,128)(2,1)S(1)}, bf16[1024,128]{1,0:T(8,128)(2,1)S(1)}, u32[]{:S(2)}, u32[]{:S(2)}) collective-permute-start(bf16[1024,128]{1,0:T(8,128)(2,1)S(1)} %get-tuple-element.12), channel_id=1, source_target_pairs={{0,128},{1,129},{2,130},{3,131},{4,0},{5,1},{6,2},{7,3},{128,132},... | collective-permute-start | bytes 786440 | tf_op jit(solution)/shard_map/ppermute | solution.py:227
  99.9 9.8 %collective-permute-start.3 = (bf16[1024,128]{1,0:T(8,128)(2,1)S(1)}, bf16[1024,128]{1,0:T(8,128)(2,1)S(1)}, u32[]{:S(2)}, u32[]{:S(2)}) collective-permute-start(bf16[1024,128]{1,0:T(8,128)(2,1)S(1)} %get-tuple-element.12), channel_id=1, source_target_pairs={{0,0},{1,1},{2,2},{3,3},{4,128},{5,129},{6,130},{7,131},{128,4},{1... | collective-permute-start | bytes 786440 | tf_op jit(solution)/shard_map/ppermute | solution.py:227
  109.7 0.7 copy-start
  110.4 1.0 copy-start.1

commit v5 on v4

--- a/solution.py
+++ b/solution.py
@@ -143,8 +143,7 @@
     )(far, *near)
 
 
-def tile_kernel(rows, chunks, xy_ref, *refs):
-    *column_refs, out_ref, narrow, left = refs
+def tile_kernel(rows, chunks, xy_ref, own_ref, other_ref, out_ref, narrow, left):
     z = lax.axis_index("z")
     x = lax.axis_index("x")
     yl = lax.axis_index("yl")
@@ -152,6 +151,7 @@
     c = plane_index()
     group = HALF * rows
     total = TILES * group
+    deep = chunks * LANES
     diagonal = c == z
     half_x = jnp.where(diagonal, 0, half_of(c, z))
     half_y = jnp.where(diagonal, 1, half_x)
@@ -168,7 +168,8 @@
     acc_y = jnp.zeros((total, LANES), F32)
     kind_x = jnp.where(diagonal, 0, 1)
     for m in range(chunks // 2):
-        columns = jnp.concatenate([column_refs[2 * m][...], column_refs[2 * m + 1][...]], axis=1)
+        half_ref, at = (own_ref, other_ref)[m // 2], m % 2 * 2 * deep
+        columns = jnp.concatenate([half_ref[at : at + deep, :], half_ref[at + deep : at + 2 * deep, :]], axis=1)
         product = jnp.dot(left[...], columns, preferred_element_type=F32)
         for n in range(2):
             k = ((core ^ (m // 2)) * 2 + ((x & 1) ^ (m % 2))) * 2 + (yl ^ n)
@@ -196,13 +197,13 @@
             out_ref[s : s + 1, :] = jnp.sum(got, axis=0, keepdims=True)
 
 
-def tile(xy, columns, rows, chunks):
+def tile(xy, own, other, rows, chunks):
     total = TILES * HALF * rows
     flops = 2 * 2 * total * (chunks * LANES) ** 2
     return pl.pallas_call(
         functools.partial(tile_kernel, rows, chunks),
         out_shape=jax.ShapeDtypeStruct((TILES, LANES), F32),
-        in_specs=[VMEM] * (1 + len(columns)),
+        in_specs=[VMEM] * 3,
         out_specs=VMEM,
         scratch_shapes=[
             pltpu.VMEM((2, chunks, total, LANES), BF16),
@@ -211,21 +212,21 @@
         cost_estimate=pl.CostEstimate(flops=flops, bytes_accessed=4_000_000, transcendentals=0),
         compiler_params=pltpu.CompilerParams(vmem_limit_bytes=16 * 1024 * 1024),
         name="tile",
-    )(xy, *columns)
+    )(xy, own, other)
 
 
 def retile(gain):
     low, yl = lax.axis_index("x") % 2, lax.axis_index("yl")
     blocks = gain.reshape(TILES // 4, -1, gain.shape[1])
     got = []
-    for a, b, n in itertools.product(range(2), repeat=3):
+    for b, n in itertools.product(range(2), repeat=2):
         turn = [
-            (((s * 2 + h) * 2 + w) * 2 + y, (((h ^ a) * 2 + s) * 2 + (w ^ b)) * 2 + (y ^ n))
+            (((s * 2 + h) * 2 + w) * 2 + y, ((h * 2 + s) * 2 + (w ^ b)) * 2 + (y ^ n))
             for s, h, w, y in itertools.product(range(2), repeat=4)
         ]
         block = lax.dynamic_index_in_dim(blocks, (low ^ b) * 2 + (yl ^ n), 0, keepdims=False)
         got.append(lax.ppermute(block, ("core", "x", "yl"), turn))
-    return got
+    return jnp.concatenate(got, axis=0)
 
 
 def shards(jacobian, gain, variance):
@@ -238,10 +239,11 @@
     near = [near[m].reshape(NEAR * rows * chunks, LANES) for m in range(QUAD)]
     for m in range(1, QUAD):
         near[m] = lax.ppermute(near[m], "z", [(s, s ^ m) for s in range(TILES)])
-    columns = retile(gain)
+    own = retile(gain)
+    other = lax.ppermute(own, "core", [(0, 1), (1, 0)])
     sent = spread(far, near, rows, chunks)
     xy = exchange(sent, PLANE)
-    partial = tile(xy, columns, rows, chunks)
+    partial = tile(xy, own, other, rows, chunks)
     in_plane = exchange(partial, PLANE).sum(axis=0)
     in_plane = in_plane[: rows * TILES].reshape(rows, TILES).transpose(1, 0)
     return variance - exchange(in_plane, "z").sum(axis=0)

time: 152 us -> 129 us (0.85)
  the two profiles are of different devices: /device:TPU:1 before, /device:TPU:2 now
where the time goes in v5:
time: 129 us; the launch traced here: 128 us
  starting transfers between devices  46.6 us (36%)
  blocking collectives  34.8 us (27%)
  waiting for transfers between devices  32.7 us (25%)
  local copies, waits for them, and re-layouts  7.42 us (6%)
  Pallas kernels  6.09 us (5%)
    all_to_all x2, blocking collectives, exchange(): return lax.all_to_all(parts, axis, split_axis=0, concat_axis=0, tiled=True)  34.8 us
    all_to_all x2, starting transfers between devices, exchange(): return lax.all_to_all(parts, axis, split_axis=0, concat_axis=0, tiled=True)  23 us
    ppermute x3, waiting for transfers between devices, shards(): near[m] = lax.ppermute(near[m], 'z', [(s, s ^ m) for s in range(TILES)])  21.4 us
    ppermute x4, starting transfers between devices, retile(): got.append(lax.ppermute(block, ('core', 'x', 'yl'), turn))  11.7 us
    ppermute x3, starting transfers between devices, shards(): near[m] = lax.ppermute(near[m], 'z', [(s, s ^ m) for s in range(TILES)])  9.99 us
    all_to_all x2, waiting for transfers between devices, exchange(): return lax.all_to_all(parts, axis, split_axis=0, concat_axis=0, tiled=True)  8.6 us
    unnamed x11, local copies, waits for them, and re-layouts  5.16 us
    pallas_call x1, Pallas kernels, spread(): pl.pallas_call(functools.partial(spread_kernel, rows, chunks), out_shape=...  2.75 us
  transfers between devices with their start and end apart: 10, of which 3 were waited for; matrix products, arithmetic and copies ran while one was open for 3% of the time, Pallas kernels for 2%

profile of v5, /device:TPU:2, one launch (start us, length us, event | category | flops | bytes accessed | tf_op | source)
XLA Modules:
  0.0 128.3 jit_solution(12009520447485885731)
XLA Ops:
  0.0 0.0 copy-start.2
  0.0 1.0 copy_bitcast_fusion.1.in_ref
  1.0 1.1 pick.1
  2.1 15.2 %all-to-all-start = ((bf16[16,7,24,128]{3,2,1,0:T(8,128)(2,1)}), bf16[16,7,24,128]{3,2,1,0:T(8,128)(2,1)S(1)}, u32[]{:S(2)}, u32[]{:S(2)}) async-start(bf16[16,7,24,128]{3,2,1,0:T(8,128)(2,1)} %get-tuple-element.7), calls=%async_computation | async-start | bytes 1376256 | tf_op jit(solution)/shard_map/all_to_all | solution.py:44
  17.4 0.0 copy-done.2
  17.4 0.1 dynamic-slice_bitcast_fusion
  17.4 3.5 %collective-permute-start.4 = (bf16[1024,128]{1,0:T(8,128)(2,1)S(1)}, bf16[1024,128]{1,0:T(8,128)(2,1)}, u32[]{:S(2)}, u32[]{:S(2)}) collective-permute-start(bf16[1024,128]{1,0:T(8,128)(2,1)S(1)} %get-tuple-element.11), channel_id=1, source_target_pairs={{0,1},{1,0},{2,3},{3,2},{4,129},{5,128},{6,131},{7,130},{128,5},{1... | collective-permute-start | bytes 786440 | tf_op jit(solution)/shard_map/ppermute | solution.py:228
  20.9 1.4 %collective-permute-start.3 = (bf16[1024,128]{1,0:T(8,128)(2,1)S(1)}, bf16[1024,128]{1,0:T(8,128)(2,1)}, u32[]{:S(2)}, u32[]{:S(2)}) collective-permute-start(bf16[1024,128]{1,0:T(8,128)(2,1)S(1)} %get-tuple-element.12), channel_id=1, source_target_pairs={{0,0},{1,1},{2,2},{3,3},{4,128},{5,129},{6,130},{7,131},{128,4},{1... | collective-permute-start | bytes 786440 | tf_op jit(solution)/shard_map/ppermute | solution.py:228
  22.3 4.7 %collective-permute-start.1 = (bf16[192,128]{1,0:T(8,128)(2,1)S(1)}, bf16[192,128]{1,0:T(8,128)(2,1)S(1)}, u32[]{:S(2)}, u32[]{:S(2)}) collective-permute-start(bf16[192,128]{1,0:T(8,128)(2,1)S(1)} %bitcast.37), channel_id=1, source_target_pairs={{0,16},{8,24},{16,0},{24,8},{32,48},{40,56},{48,32},{56,40},{64,80... | collective-permute-start | bytes 147464 | tf_op jit(solution)/shard_map/ppermute | solution.py:241
  27.0 3.4 %collective-permute-start.2 = (bf16[192,128]{1,0:T(8,128)(2,1)S(1)}, bf16[192,128]{1,0:T(8,128)(2,1)S(1)}, u32[]{:S(2)}, u32[]{:S(2)}) collective-permute-start(bf16[192,128]{1,0:T(8,128)(2,1)S(1)} %bitcast.36), channel_id=1, source_target_pairs={{0,24},{8,16},{16,8},{24,0},{32,56},{40,48},{48,40},{56,32},{64,88... | collective-permute-start | bytes 147464 | tf_op jit(solution)/shard_map/ppermute | solution.py:241
  30.4 1.9 %collective-permute-start = (bf16[192,128]{1,0:T(8,128)(2,1)S(1)}, bf16[192,128]{1,0:T(8,128)(2,1)S(1)}, u32[]{:S(2)}, u32[]{:S(2)}) collective-permute-start(bf16[192,128]{1,0:T(8,128)(2,1)S(1)} %bitcast.35), channel_id=1, source_target_pairs={{0,8},{8,0},{16,24},{24,16},{32,40},{40,32},{48,56},{56,48},{64,72... | collective-permute-start | bytes 147464 | tf_op jit(solution)/shard_map/ppermute | solution.py:241
  32.3 21.4 %collective-permute-done.1.refs_2_ = bf16[192,128]{1,0:T(8,128)(2,1)S(1)} collective-permute-done((bf16[192,128]{1,0:T(8,128)(2,1)S(1)}, bf16[192,128]{1,0:T(8,128)(2,1)S(1)}, u32[]{:S(2)}, u32[]{:S(2)}) %collective-permute-start.1) | collective-permute-done | bytes 49184 | tf_op jit(solution)/shard_map/ppermute | solution.py:241
  53.7 2.4 %collective-permute-start.5 = (bf16[1024,128]{1,0:T(8,128)(2,1)S(1)}, bf16[1024,128]{1,0:T(8,128)(2,1)}, u32[]{:S(2)}, u32[]{:S(2)}) collective-permute-start(bf16[1024,128]{1,0:T(8,128)(2,1)S(1)} %get-tuple-element.10), channel_id=1, source_target_pairs={{0,2},{1,3},{2,0},{3,1},{4,130},{5,131},{6,128},{7,129},{128,6},{1... | collective-permute-start | bytes 786440 | tf_op jit(solution)/shard_map/ppermute | solution.py:228
  56.2 0.0 collective-permute-done.2.refs_3_
  56.2 4.4 %collective-permute-start.6 = (bf16[1024,128]{1,0:T(8,128)(2,1)S(1)}, bf16[1024,128]{1,0:T(8,128)(2,1)}, u32[]{:S(2)}, u32[]{:S(2)}) collective-permute-start(bf16[1024,128]{1,0:T(8,128)(2,1)S(1)} %get-tuple-element.9), channel_id=1, source_target_pairs={{0,3},{1,2},{2,1},{3,0},{4,131},{5,130},{6,129},{7,128},{128,7},{1... | collective-permute-start | bytes 786440 | tf_op jit(solution)/shard_map/ppermute | solution.py:228
  60.6 0.0 collective-permute-done.refs_1_
  60.6 0.0 all-to-all-done
  60.6 2.7 %spread.1 = bf16[16,16,24,128]{3,2,1,0:T(8,128)(2,1)} custom-call(bf16[16,168,128]{2,1,0:T(8,128)(2,1)S(1)} %bitcast.30, bf16[192,128]{1,0:T(8,128)(2,1)S(1)} %bitcast.31, bf16[192,128]{1,0:T(8,128)(2,1)S(1)} %collective-permute-done.refs_1_, bf16[192,128]{1,0:T(8,128)(2,1)S(1)} %collective-permute-done.1.refs_2_, ...), custom_call_target="tpu_custom_call" | custom-call | flops 4000000 | bytes 2500000 | tf_op jit(solution)/shard_map/spread/pallas_call | solution.py:131
  63.4 7.8 %all-to-all-start.1 = ((bf16[16,16,24,128]{3,2,1,0:T(8,128)(2,1)}), bf16[16,16,24,128]{3,2,1,0:T(8,128)(2,1)S(1)}, u32[]{:S(2)}, u32[]{:S(2)}) async-start(bf16[16,16,24,128]{3,2,1,0:T(8,128)(2,1)} %spread.1), calls=%async_computation.1 | async-start | bytes 3145728 | tf_op jit(solution)/shard_map/all_to_all | solution.py:44
  71.2 0.0 collective-permute-done.3
  71.2 1.0 constant_dynamic-update-slice_fusion.3
  72.2 0.0 collective-permute-done.4
  72.2 1.0 constant_dynamic-update-slice_fusion.2
  73.2 0.0 collective-permute-done.5
  73.2 1.0 constant_dynamic-update-slice_fusion.1
  74.2 0.0 collective-permute-done.6
  74.2 0.0 copy-start.3
  74.2 1.0 constant_dynamic-update-slice_fusion.own_ref
  75.2 1.9 %collective-permute-start.7 = (bf16[4096,128]{1,0:T(8,128)(2,1)S(1)}, bf16[4096,128]{1,0:T(8,128)(2,1)S(1)}, u32[]{:S(2)}, u32[]{:S(2)}) collective-permute-start(bf16[4096,128]{1,0:T(8,128)(2,1)S(1)} %constant_dynamic-update-slice_fusion.own_ref), channel_id=1, source_target_pairs={{0,128},{128,0},{1,129},{129,1},{2,130},{130,2},{3,131},{131,3},{4... | collective-permute-start | bytes 3145736 | tf_op jit(solution)/shard_map/ppermute | solution.py:243
  77.2 2.6 %collective-permute-done.7.other_ref = bf16[4096,128]{1,0:T(8,128)(2,1)S(1)} collective-permute-done((bf16[4096,128]{1,0:T(8,128)(2,1)S(1)}, bf16[4096,128]{1,0:T(8,128)(2,1)S(1)}, u32[]{:S(2)}, u32[]{:S(2)}) %collective-permute-start.7) | collective-permute-done | bytes 1048608 | tf_op jit(solution)/shard_map/ppermute | solution.py:243
  79.8 0.0 copy-start
  79.8 1.0 copy-done
  80.8 8.6 %all-to-all-done.1.xy_ref = bf16[16,16,24,128]{3,2,1,0:T(8,128)(2,1)S(1)} async-done(((bf16[16,16,24,128]{3,2,1,0:T(8,128)(2,1)}), bf16[16,16,24,128]{3,2,1,0:T(8,128)(2,1)S(1)}, u32[]{:S(2)}, u32[]{:S(2)}) %all-to-all-start.1) | async-done | bytes 1572896 | tf_op jit(solution)/shard_map/all_to_all | solution.py:44
  89.4 0.0 copy-start.1
  89.4 1.2 copy-done.1
  90.6 2.2 %tile.1 = f32[16,128]{1,0:T(8,128)S(1)} custom-call(bf16[16,16,24,128]{3,2,1,0:T(8,128)(2,1)S(1)} %all-to-all-done.1.xy_ref, bf16[4096,128]{1,0:T(8,128)(2,1)S(1)} %constant_dynamic-update-slice_fusion.own_ref, bf16[4096,128]{1,0:T(8,128)(2,1)S(1)} %copy-done.1), custom_call_target="tpu_custom_call" | custom-call | flops 1610612736 | bytes 4000000 | tf_op jit(solution)/shard_map/tile/pallas_call | solution.py:203
  92.8 12.4 %all_to_all.28 = f32[16,1,128]{2,1,0:T(1,128)S(1)} all-to-all(f32[16,1,128]{2,1,0:T(1,128)S(1)} %bitcast.32), channel_id=1, replica_groups=mesh['yh'=2,'core'=2,'z'=16,'x'=4,'yl'=2] {'yh','x','yl'}, dimensions={0} | all-to-all | bytes 16384 | tf_op jit(solution)/shard_map/all_to_all | solution.py:44
  105.2 0.1 reshape.31
  105.3 0.1 copy.7
  105.4 22.4 %all_to_all.29 = f32[16,1,3]{2,1,0:T(1,128)S(1)} all-to-all(f32[16,1,3]{2,1,0:T(1,128)S(1)} %copy.7), channel_id=1, replica_groups=mesh['yh'=2,'core'=2,'z'=16,'x'=4,'yl'=2] {'z'}, dimensions={0} | all-to-all | bytes 384 | tf_op jit(solution)/shard_map/all_to_all | solution.py:44
  127.8 0.0 copy-done.3
  127.8 0.5 sub.3
  (3 shorter events, 0.1 us)
Async XLA Ops:
  0.0 17.4 %copy-start.2 = (bf16[4096,128]{1,0:T(8,128)(2,1)S(1)}, bf16[4096,128]{1,0:T(8,128)(2,1)}, u32[]{:S(2)}) copy-start(bf16[4096,128]{1,0:T(8,128)(2,1)} %param.4) | copy-start | bytes 3145732
  2.1 58.5 %all-to-all-start = ((bf16[16,7,24,128]{3,2,1,0:T(8,128)(2,1)}), bf16[16,7,24,128]{3,2,1,0:T(8,128)(2,1)S(1)}, u32[]{:S(2)}, u32[]{:S(2)}) async-start(bf16[16,7,24,128]{3,2,1,0:T(8,128)(2,1)} %get-tuple-element.7), calls=%async_computation | async-start | bytes 1376256 | tf_op jit(solution)/shard_map/all_to_all | solution.py:44
  17.4 54.8 %collective-permute-start.4 = (bf16[1024,128]{1,0:T(8,128)(2,1)S(1)}, bf16[1024,128]{1,0:T(8,128)(2,1)}, u32[]{:S(2)}, u32[]{:S(2)}) collective-permute-start(bf16[1024,128]{1,0:T(8,128)(2,1)S(1)} %get-tuple-element.11), channel_id=1, source_target_pairs={{0,1},{1,0},{2,3},{3,2},{4,129},{5,128},{6,131},{7,130},{128,5},{1... | collective-permute-start | bytes 786440 | tf_op jit(solution)/shard_map/ppermute | solution.py:228
  20.9 50.3 %collective-permute-start.3 = (bf16[1024,128]{1,0:T(8,128)(2,1)S(1)}, bf16[1024,128]{1,0:T(8,128)(2,1)}, u32[]{:S(2)}, u32[]{:S(2)}) collective-permute-start(bf16[1024,128]{1,0:T(8,128)(2,1)S(1)} %get-tuple-element.12), channel_id=1, source_target_pairs={{0,0},{1,1},{2,2},{3,3},{4,128},{5,129},{6,130},{7,131},{128,4},{1... | collective-permute-start | bytes 786440 | tf_op jit(solution)/shard_map/ppermute | solution.py:228
  22.3 31.4 %collective-permute-start.1 = (bf16[192,128]{1,0:T(8,128)(2,1)S(1)}, bf16[192,128]{1,0:T(8,128)(2,1)S(1)}, u32[]{:S(2)}, u32[]{:S(2)}) collective-permute-start(bf16[192,128]{1,0:T(8,128)(2,1)S(1)} %bitcast.37), channel_id=1, source_target_pairs={{0,16},{8,24},{16,0},{24,8},{32,48},{40,56},{48,32},{56,40},{64,80... | collective-permute-start | bytes 147464 | tf_op jit(solution)/shard_map/ppermute | solution.py:241
  27.0 29.2 %collective-permute-start.2 = (bf16[192,128]{1,0:T(8,128)(2,1)S(1)}, bf16[192,128]{1,0:T(8,128)(2,1)S(1)}, u32[]{:S(2)}, u32[]{:S(2)}) collective-permute-start(bf16[192,128]{1,0:T(8,128)(2,1)S(1)} %bitcast.36), channel_id=1, source_target_pairs={{0,24},{8,16},{16,8},{24,0},{32,56},{40,48},{48,40},{56,32},{64,88... | collective-permute-start | bytes 147464 | tf_op jit(solution)/shard_map/ppermute | solution.py:241
  30.4 30.2 %collective-permute-start = (bf16[192,128]{1,0:T(8,128)(2,1)S(1)}, bf16[192,128]{1,0:T(8,128)(2,1)S(1)}, u32[]{:S(2)}, u32[]{:S(2)}) collective-permute-start(bf16[192,128]{1,0:T(8,128)(2,1)S(1)} %bitcast.35), channel_id=1, source_target_pairs={{0,8},{8,0},{16,24},{24,16},{32,40},{40,32},{48,56},{56,48},{64,72... | collective-permute-start | bytes 147464 | tf_op jit(solution)/shard_map/ppermute | solution.py:241
  53.7 19.5 %collective-permute-start.5 = (bf16[1024,128]{1,0:T(8,128)(2,1)S(1)}, bf16[1024,128]{1,0:T(8,128)(2,1)}, u32[]{:S(2)}, u32[]{:S(2)}) collective-permute-start(bf16[1024,128]{1,0:T(8,128)(2,1)S(1)} %get-tuple-element.10), channel_id=1, source_target_pairs={{0,2},{1,3},{2,0},{3,1},{4,130},{5,131},{6,128},{7,129},{128,6},{1... | collective-permute-start | bytes 786440 | tf_op jit(solution)/shard_map/ppermute | solution.py:228
  56.2 18.0 %collective-permute-start.6 = (bf16[1024,128]{1,0:T(8,128)(2,1)S(1)}, bf16[1024,128]{1,0:T(8,128)(2,1)}, u32[]{:S(2)}, u32[]{:S(2)}) collective-permute-start(bf16[1024,128]{1,0:T(8,128)(2,1)S(1)} %get-tuple-element.9), channel_id=1, source_target_pairs={{0,3},{1,2},{2,1},{3,0},{4,131},{5,130},{6,129},{7,128},{128,7},{1... | collective-permute-start | bytes 786440 | tf_op jit(solution)/shard_map/ppermute | solution.py:228
  63.4 26.0 %all-to-all-start.1 = ((bf16[16,16,24,128]{3,2,1,0:T(8,128)(2,1)}), bf16[16,16,24,128]{3,2,1,0:T(8,128)(2,1)S(1)}, u32[]{:S(2)}, u32[]{:S(2)}) async-start(bf16[16,16,24,128]{3,2,1,0:T(8,128)(2,1)} %spread.1), calls=%async_computation.1 | async-start | bytes 3145728 | tf_op jit(solution)/shard_map/all_to_all | solution.py:44
  74.2 53.6 %copy-start.3 = (f32[3]{0:T(128)S(1)}, f32[3]{0:T(128)}, u32[]{:S(2)}) copy-start(f32[3]{0:T(128)} %param.5) | copy-start | bytes 40
  75.2 4.6 %collective-permute-start.7 = (bf16[4096,128]{1,0:T(8,128)(2,1)S(1)}, bf16[4096,128]{1,0:T(8,128)(2,1)S(1)}, u32[]{:S(2)}, u32[]{:S(2)}) collective-permute-start(bf16[4096,128]{1,0:T(8,128)(2,1)S(1)} %constant_dynamic-update-slice_fusion.own_ref), channel_id=1, source_target_pairs={{0,128},{128,0},{1,129},{129,1},{2,130},{130,2},{3,131},{131,3},{4... | collective-permute-start | bytes 3145736 | tf_op jit(solution)/shard_map/ppermute | solution.py:243
  79.8 1.0 copy-start
  89.4 1.2 copy-start.1

commit v6 on v5

--- a/solution.py
+++ b/solution.py
@@ -90,7 +90,7 @@
         at = near_at + m * NEAR * block
         wide[at : at + NEAR * block, :] = near_refs[m][...].astype(F32)
 
-    @pl.loop(0, TILES)
+    @pl.loop(0, TILES, unroll=4)
     def _(to):
         diagonal = to == z
         quad = to // QUAD
@@ -143,7 +143,7 @@
     )(far, *near)
 
 
-def tile_kernel(rows, chunks, xy_ref, own_ref, other_ref, out_ref, narrow, left):
+def tile_kernel(rows, chunks, xy_ref, own_ref, other_ref, out_ref, left):
     z = lax.axis_index("z")
     x = lax.axis_index("x")
     yl = lax.axis_index("yl")
@@ -163,10 +163,9 @@
                 start = kind * total + s * group
                 got = xy_ref[s, kind * chunks + q]
                 left[start : start + group, lane : lane + LANES] = got
-                narrow[kind, q, s * group : (s + 1) * group, :] = got
     acc_x = jnp.zeros((total, LANES), F32)
     acc_y = jnp.zeros((total, LANES), F32)
-    kind_x = jnp.where(diagonal, 0, 1)
+    top_x = pl.multiple_of(jnp.where(diagonal, 0, total), HALF)
     for m in range(chunks // 2):
         half_ref, at = (own_ref, other_ref)[m // 2], m % 2 * 2 * deep
         columns = jnp.concatenate([half_ref[at : at + deep, :], half_ref[at + deep : at + 2 * deep, :]], axis=1)
@@ -174,13 +173,10 @@
         for n in range(2):
             k = ((core ^ (m // 2)) * 2 + ((x & 1) ^ (m % 2))) * 2 + (yl ^ n)
             part = product[:, n * LANES : (n + 1) * LANES]
-            acc_x += part[:total] * narrow[kind_x, k].astype(F32)
-            acc_y += part[total:] * narrow[1, k].astype(F32)
-    ones = jnp.ones((LANES, LANES), F32)
-    sum_x, sum_y = (
-        jnp.dot(acc, ones, precision=lax.Precision.HIGHEST, preferred_element_type=F32)
-        for acc in (acc_x, acc_y)
-    )
+            lanes = pl.ds(pl.multiple_of(k * LANES, LANES), LANES)
+            acc_x += part[:total] * left[pl.ds(top_x, total), lanes].astype(F32)
+            acc_y += part[total:] * left[total:, lanes].astype(F32)
+    sum_x, sum_y = (jnp.sum(acc, axis=1, keepdims=True) for acc in (acc_x, acc_y))
     lane = lax.broadcasted_iota(jnp.int32, (group, LANES), 1)
     row = lax.broadcasted_iota(jnp.int32, (group, LANES), 0)
     r, k = row // HALF, row % HALF
@@ -206,7 +202,6 @@
         in_specs=[VMEM] * 3,
         out_specs=VMEM,
         scratch_shapes=[
-            pltpu.VMEM((2, chunks, total, LANES), BF16),
             pltpu.VMEM((2 * total, chunks * LANES), BF16),
         ],
         cost_estimate=pl.CostEstimate(flops=flops, bytes_accessed=4_000_000, transcendentals=0),

time: 129 us -> 129 us (level)
  no operation moved by 1% of the time
where the time goes in v6:
time: 129 us; the launch traced here: 128 us
  starting transfers between devices  46.6 us (36%)
  blocking collectives  34.8 us (27%)
  waiting for transfers between devices  32.7 us (25%)
  local copies, waits for them, and re-layouts  7.42 us (6%)
  Pallas kernels  5.6 us (4%)
    all_to_all x2, blocking collectives, exchange(): return lax.all_to_all(parts, axis, split_axis=0, concat_axis=0, tiled=True)  34.8 us
    all_to_all x2, starting transfers between devices, exchange(): return lax.all_to_all(parts, axis, split_axis=0, concat_axis=0, tiled=True)  23 us
    ppermute x3, waiting for transfers between devices, shards(): near[m] = lax.ppermute(near[m], 'z', [(s, s ^ m) for s in range(TILES)])  21.4 us
    ppermute x4, starting transfers between devices, retile(): got.append(lax.ppermute(block, ('core', 'x', 'yl'), turn))  11.7 us
    ppermute x3, starting transfers between devices, shards(): near[m] = lax.ppermute(near[m], 'z', [(s, s ^ m) for s in range(TILES)])  9.99 us
    all_to_all x2, waiting for transfers between devices, exchange(): return lax.all_to_all(parts, axis, split_axis=0, concat_axis=0, tiled=True)  8.6 us
    unnamed x11, local copies, waits for them, and re-layouts  5.16 us
    ppermute x1, waiting for transfers between devices, shards(): other = lax.ppermute(own, 'core', [(0, 1), (1, 0)])  2.63 us
  transfers between devices with their start and end apart: 10, of which 3 were waited for; matrix products, arithmetic and copies ran while one was open for 3% of the time, Pallas kernels for 2%

profile of v6, /device:TPU:2, one launch (start us, length us, event | category | flops | bytes accessed | tf_op | source)
XLA Modules:
  0.0 127.9 jit_solution(2810703614031188000)
XLA Ops:
  0.0 0.0 copy-start.2
  0.0 1.0 copy_bitcast_fusion.1.in_ref
  1.0 1.1 pick.1
  2.1 15.2 %all-to-all-start = ((bf16[16,7,24,128]{3,2,1,0:T(8,128)(2,1)}), bf16[16,7,24,128]{3,2,1,0:T(8,128)(2,1)S(1)}, u32[]{:S(2)}, u32[]{:S(2)}) async-start(bf16[16,7,24,128]{3,2,1,0:T(8,128)(2,1)} %get-tuple-element.7), calls=%async_computation | async-start | bytes 1376256 | tf_op jit(solution)/shard_map/all_to_all | solution.py:44
  17.4 0.0 copy-done.2
  17.4 0.1 dynamic-slice_bitcast_fusion
  17.4 3.5 %collective-permute-start.4 = (bf16[1024,128]{1,0:T(8,128)(2,1)S(1)}, bf16[1024,128]{1,0:T(8,128)(2,1)}, u32[]{:S(2)}, u32[]{:S(2)}) collective-permute-start(bf16[1024,128]{1,0:T(8,128)(2,1)S(1)} %get-tuple-element.11), channel_id=1, source_target_pairs={{0,1},{1,0},{2,3},{3,2},{4,129},{5,128},{6,131},{7,130},{128,5},{1... | collective-permute-start | bytes 786440 | tf_op jit(solution)/shard_map/ppermute | solution.py:223
  20.9 1.4 %collective-permute-start.3 = (bf16[1024,128]{1,0:T(8,128)(2,1)S(1)}, bf16[1024,128]{1,0:T(8,128)(2,1)}, u32[]{:S(2)}, u32[]{:S(2)}) collective-permute-start(bf16[1024,128]{1,0:T(8,128)(2,1)S(1)} %get-tuple-element.12), channel_id=1, source_target_pairs={{0,0},{1,1},{2,2},{3,3},{4,128},{5,129},{6,130},{7,131},{128,4},{1... | collective-permute-start | bytes 786440 | tf_op jit(solution)/shard_map/ppermute | solution.py:223
  22.3 4.7 %collective-permute-start.1 = (bf16[192,128]{1,0:T(8,128)(2,1)S(1)}, bf16[192,128]{1,0:T(8,128)(2,1)S(1)}, u32[]{:S(2)}, u32[]{:S(2)}) collective-permute-start(bf16[192,128]{1,0:T(8,128)(2,1)S(1)} %bitcast.37), channel_id=1, source_target_pairs={{0,16},{8,24},{16,0},{24,8},{32,48},{40,56},{48,32},{56,40},{64,80... | collective-permute-start | bytes 147464 | tf_op jit(solution)/shard_map/ppermute | solution.py:236
  27.0 3.4 %collective-permute-start.2 = (bf16[192,128]{1,0:T(8,128)(2,1)S(1)}, bf16[192,128]{1,0:T(8,128)(2,1)S(1)}, u32[]{:S(2)}, u32[]{:S(2)}) collective-permute-start(bf16[192,128]{1,0:T(8,128)(2,1)S(1)} %bitcast.36), channel_id=1, source_target_pairs={{0,24},{8,16},{16,8},{24,0},{32,56},{40,48},{48,40},{56,32},{64,88... | collective-permute-start | bytes 147464 | tf_op jit(solution)/shard_map/ppermute | solution.py:236
  30.4 1.9 %collective-permute-start = (bf16[192,128]{1,0:T(8,128)(2,1)S(1)}, bf16[192,128]{1,0:T(8,128)(2,1)S(1)}, u32[]{:S(2)}, u32[]{:S(2)}) collective-permute-start(bf16[192,128]{1,0:T(8,128)(2,1)S(1)} %bitcast.35), channel_id=1, source_target_pairs={{0,8},{8,0},{16,24},{24,16},{32,40},{40,32},{48,56},{56,48},{64,72... | collective-permute-start | bytes 147464 | tf_op jit(solution)/shard_map/ppermute | solution.py:236
  32.3 21.4 %collective-permute-done.1.refs_2_ = bf16[192,128]{1,0:T(8,128)(2,1)S(1)} collective-permute-done((bf16[192,128]{1,0:T(8,128)(2,1)S(1)}, bf16[192,128]{1,0:T(8,128)(2,1)S(1)}, u32[]{:S(2)}, u32[]{:S(2)}) %collective-permute-start.1) | collective-permute-done | bytes 49184 | tf_op jit(solution)/shard_map/ppermute | solution.py:236
  53.7 2.4 %collective-permute-start.5 = (bf16[1024,128]{1,0:T(8,128)(2,1)S(1)}, bf16[1024,128]{1,0:T(8,128)(2,1)}, u32[]{:S(2)}, u32[]{:S(2)}) collective-permute-start(bf16[1024,128]{1,0:T(8,128)(2,1)S(1)} %get-tuple-element.10), channel_id=1, source_target_pairs={{0,2},{1,3},{2,0},{3,1},{4,130},{5,131},{6,128},{7,129},{128,6},{1... | collective-permute-start | bytes 786440 | tf_op jit(solution)/shard_map/ppermute | solution.py:223
  56.2 0.0 collective-permute-done.2.refs_3_
  56.2 4.4 %collective-permute-start.6 = (bf16[1024,128]{1,0:T(8,128)(2,1)S(1)}, bf16[1024,128]{1,0:T(8,128)(2,1)}, u32[]{:S(2)}, u32[]{:S(2)}) collective-permute-start(bf16[1024,128]{1,0:T(8,128)(2,1)S(1)} %get-tuple-element.9), channel_id=1, source_target_pairs={{0,3},{1,2},{2,1},{3,0},{4,131},{5,130},{6,129},{7,128},{128,7},{1... | collective-permute-start | bytes 786440 | tf_op jit(solution)/shard_map/ppermute | solution.py:223
  60.6 0.0 collective-permute-done.refs_1_
  60.6 0.0 all-to-all-done
  60.6 2.6 %spread.1 = bf16[16,16,24,128]{3,2,1,0:T(8,128)(2,1)} custom-call(bf16[16,168,128]{2,1,0:T(8,128)(2,1)S(1)} %bitcast.30, bf16[192,128]{1,0:T(8,128)(2,1)S(1)} %bitcast.31, bf16[192,128]{1,0:T(8,128)(2,1)S(1)} %collective-permute-done.refs_1_, bf16[192,128]{1,0:T(8,128)(2,1)S(1)} %collective-permute-done.1.refs_2_, ...), custom_call_target="tpu_custom_call" | custom-call | flops 4000000 | bytes 2500000 | tf_op jit(solution)/shard_map/spread/pallas_call | solution.py:131
  63.2 7.8 %all-to-all-start.1 = ((bf16[16,16,24,128]{3,2,1,0:T(8,128)(2,1)}), bf16[16,16,24,128]{3,2,1,0:T(8,128)(2,1)S(1)}, u32[]{:S(2)}, u32[]{:S(2)}) async-start(bf16[16,16,24,128]{3,2,1,0:T(8,128)(2,1)} %spread.1), calls=%async_computation.1 | async-start | bytes 3145728 | tf_op jit(solution)/shard_map/all_to_all | solution.py:44
  71.1 0.0 collective-permute-done.3
  71.1 1.0 constant_dynamic-update-slice_fusion.3
  72.0 0.0 collective-permute-done.4
  72.1 1.0 constant_dynamic-update-slice_fusion.2
  73.0 0.0 collective-permute-done.5
  73.1 1.0 constant_dynamic-update-slice_fusion.1
  74.0 0.0 collective-permute-done.6
  74.1 0.0 copy-start.3
  74.1 1.0 constant_dynamic-update-slice_fusion.own_ref
  75.1 1.9 %collective-permute-start.7 = (bf16[4096,128]{1,0:T(8,128)(2,1)S(1)}, bf16[4096,128]{1,0:T(8,128)(2,1)S(1)}, u32[]{:S(2)}, u32[]{:S(2)}) collective-permute-start(bf16[4096,128]{1,0:T(8,128)(2,1)S(1)} %constant_dynamic-update-slice_fusion.own_ref), channel_id=1, source_target_pairs={{0,128},{128,0},{1,129},{129,1},{2,130},{130,2},{3,131},{131,3},{4... | collective-permute-start | bytes 3145736 | tf_op jit(solution)/shard_map/ppermute | solution.py:238
  77.0 2.6 %collective-permute-done.7.other_ref = bf16[4096,128]{1,0:T(8,128)(2,1)S(1)} collective-permute-done((bf16[4096,128]{1,0:T(8,128)(2,1)S(1)}, bf16[4096,128]{1,0:T(8,128)(2,1)S(1)}, u32[]{:S(2)}, u32[]{:S(2)}) %collective-permute-start.7) | collective-permute-done | bytes 1048608 | tf_op jit(solution)/shard_map/ppermute | solution.py:238
  79.6 0.0 copy-start
  79.6 1.0 copy-done
  80.6 8.6 %all-to-all-done.1.xy_ref = bf16[16,16,24,128]{3,2,1,0:T(8,128)(2,1)S(1)} async-done(((bf16[16,16,24,128]{3,2,1,0:T(8,128)(2,1)}), bf16[16,16,24,128]{3,2,1,0:T(8,128)(2,1)S(1)}, u32[]{:S(2)}, u32[]{:S(2)}) %all-to-all-start.1) | async-done | bytes 1572896 | tf_op jit(solution)/shard_map/all_to_all | solution.py:44
  89.2 0.0 copy-start.1
  89.2 1.2 copy-done.1
  90.4 1.9 %tile.1 = f32[16,128]{1,0:T(8,128)S(1)} custom-call(bf16[16,16,24,128]{3,2,1,0:T(8,128)(2,1)S(1)} %all-to-all-done.1.xy_ref, bf16[4096,128]{1,0:T(8,128)(2,1)S(1)} %constant_dynamic-update-slice_fusion.own_ref, bf16[4096,128]{1,0:T(8,128)(2,1)S(1)} %copy-done.1), custom_call_target="tpu_custom_call" | custom-call | flops 1610612736 | bytes 4000000 | tf_op jit(solution)/shard_map/tile/pallas_call | solution.py:199
  92.4 12.4 %all_to_all.28 = f32[16,1,128]{2,1,0:T(1,128)S(1)} all-to-all(f32[16,1,128]{2,1,0:T(1,128)S(1)} %bitcast.32), channel_id=1, replica_groups=mesh['yh'=2,'core'=2,'z'=16,'x'=4,'yl'=2] {'yh','x','yl'}, dimensions={0} | all-to-all | bytes 16384 | tf_op jit(solution)/shard_map/all_to_all | solution.py:44
  104.7 0.1 reshape.31
  104.8 0.1 copy.7
  104.9 22.4 %all_to_all.29 = f32[16,1,3]{2,1,0:T(1,128)S(1)} all-to-all(f32[16,1,3]{2,1,0:T(1,128)S(1)} %copy.7), channel_id=1, replica_groups=mesh['yh'=2,'core'=2,'z'=16,'x'=4,'yl'=2] {'z'}, dimensions={0} | all-to-all | bytes 384 | tf_op jit(solution)/shard_map/all_to_all | solution.py:44
  127.4 0.0 copy-done.3
  127.4 0.5 sub.3
  (3 shorter events, 0.1 us)
Async XLA Ops:
  0.0 17.4 %copy-start.2 = (bf16[4096,128]{1,0:T(8,128)(2,1)S(1)}, bf16[4096,128]{1,0:T(8,128)(2,1)}, u32[]{:S(2)}) copy-start(bf16[4096,128]{1,0:T(8,128)(2,1)} %param.4) | copy-start | bytes 3145732
  2.1 58.5 %all-to-all-start = ((bf16[16,7,24,128]{3,2,1,0:T(8,128)(2,1)}), bf16[16,7,24,128]{3,2,1,0:T(8,128)(2,1)S(1)}, u32[]{:S(2)}, u32[]{:S(2)}) async-start(bf16[16,7,24,128]{3,2,1,0:T(8,128)(2,1)} %get-tuple-element.7), calls=%async_computation | async-start | bytes 1376256 | tf_op jit(solution)/shard_map/all_to_all | solution.py:44
  17.4 54.6 %collective-permute-start.4 = (bf16[1024,128]{1,0:T(8,128)(2,1)S(1)}, bf16[1024,128]{1,0:T(8,128)(2,1)}, u32[]{:S(2)}, u32[]{:S(2)}) collective-permute-start(bf16[1024,128]{1,0:T(8,128)(2,1)S(1)} %get-tuple-element.11), channel_id=1, source_target_pairs={{0,1},{1,0},{2,3},{3,2},{4,129},{5,128},{6,131},{7,130},{128,5},{1... | collective-permute-start | bytes 786440 | tf_op jit(solution)/shard_map/ppermute | solution.py:223
  20.9 50.1 %collective-permute-start.3 = (bf16[1024,128]{1,0:T(8,128)(2,1)S(1)}, bf16[1024,128]{1,0:T(8,128)(2,1)}, u32[]{:S(2)}, u32[]{:S(2)}) collective-permute-start(bf16[1024,128]{1,0:T(8,128)(2,1)S(1)} %get-tuple-element.12), channel_id=1, source_target_pairs={{0,0},{1,1},{2,2},{3,3},{4,128},{5,129},{6,130},{7,131},{128,4},{1... | collective-permute-start | bytes 786440 | tf_op jit(solution)/shard_map/ppermute | solution.py:223
  22.3 31.4 %collective-permute-start.1 = (bf16[192,128]{1,0:T(8,128)(2,1)S(1)}, bf16[192,128]{1,0:T(8,128)(2,1)S(1)}, u32[]{:S(2)}, u32[]{:S(2)}) collective-permute-start(bf16[192,128]{1,0:T(8,128)(2,1)S(1)} %bitcast.37), channel_id=1, source_target_pairs={{0,16},{8,24},{16,0},{24,8},{32,48},{40,56},{48,32},{56,40},{64,80... | collective-permute-start | bytes 147464 | tf_op jit(solution)/shard_map/ppermute | solution.py:236
  27.0 29.2 %collective-permute-start.2 = (bf16[192,128]{1,0:T(8,128)(2,1)S(1)}, bf16[192,128]{1,0:T(8,128)(2,1)S(1)}, u32[]{:S(2)}, u32[]{:S(2)}) collective-permute-start(bf16[192,128]{1,0:T(8,128)(2,1)S(1)} %bitcast.36), channel_id=1, source_target_pairs={{0,24},{8,16},{16,8},{24,0},{32,56},{40,48},{48,40},{56,32},{64,88... | collective-permute-start | bytes 147464 | tf_op jit(solution)/shard_map/ppermute | solution.py:236
  30.4 30.2 %collective-permute-start = (bf16[192,128]{1,0:T(8,128)(2,1)S(1)}, bf16[192,128]{1,0:T(8,128)(2,1)S(1)}, u32[]{:S(2)}, u32[]{:S(2)}) collective-permute-start(bf16[192,128]{1,0:T(8,128)(2,1)S(1)} %bitcast.35), channel_id=1, source_target_pairs={{0,8},{8,0},{16,24},{24,16},{32,40},{40,32},{48,56},{56,48},{64,72... | collective-permute-start | bytes 147464 | tf_op jit(solution)/shard_map/ppermute | solution.py:236
  53.7 19.3 %collective-permute-start.5 = (bf16[1024,128]{1,0:T(8,128)(2,1)S(1)}, bf16[1024,128]{1,0:T(8,128)(2,1)}, u32[]{:S(2)}, u32[]{:S(2)}) collective-permute-start(bf16[1024,128]{1,0:T(8,128)(2,1)S(1)} %get-tuple-element.10), channel_id=1, source_target_pairs={{0,2},{1,3},{2,0},{3,1},{4,130},{5,131},{6,128},{7,129},{128,6},{1... | collective-permute-start | bytes 786440 | tf_op jit(solution)/shard_map/ppermute | solution.py:223
  56.2 17.8 %collective-permute-start.6 = (bf16[1024,128]{1,0:T(8,128)(2,1)S(1)}, bf16[1024,128]{1,0:T(8,128)(2,1)}, u32[]{:S(2)}, u32[]{:S(2)}) collective-permute-start(bf16[1024,128]{1,0:T(8,128)(2,1)S(1)} %get-tuple-element.9), channel_id=1, source_target_pairs={{0,3},{1,2},{2,1},{3,0},{4,131},{5,130},{6,129},{7,128},{128,7},{1... | collective-permute-start | bytes 786440 | tf_op jit(solution)/shard_map/ppermute | solution.py:223
  63.2 26.0 %all-to-all-start.1 = ((bf16[16,16,24,128]{3,2,1,0:T(8,128)(2,1)}), bf16[16,16,24,128]{3,2,1,0:T(8,128)(2,1)S(1)}, u32[]{:S(2)}, u32[]{:S(2)}) async-start(bf16[16,16,24,128]{3,2,1,0:T(8,128)(2,1)} %spread.1), calls=%async_computation.1 | async-start | bytes 3145728 | tf_op jit(solution)/shard_map/all_to_all | solution.py:44
  74.1 53.3 %copy-start.3 = (f32[3]{0:T(128)S(1)}, f32[3]{0:T(128)}, u32[]{:S(2)}) copy-start(f32[3]{0:T(128)} %param.5) | copy-start | bytes 40
  75.1 4.6 %collective-permute-start.7 = (bf16[4096,128]{1,0:T(8,128)(2,1)S(1)}, bf16[4096,128]{1,0:T(8,128)(2,1)S(1)}, u32[]{:S(2)}, u32[]{:S(2)}) collective-permute-start(bf16[4096,128]{1,0:T(8,128)(2,1)S(1)} %constant_dynamic-update-slice_fusion.own_ref), channel_id=1, source_target_pairs={{0,128},{128,0},{1,129},{129,1},{2,130},{130,2},{3,131},{131,3},{4... | collective-permute-start | bytes 3145736 | tf_op jit(solution)/shard_map/ppermute | solution.py:238
  79.6 1.0 copy-start
  89.2 1.2 copy-start.1
